TPU v7x, 8 devices: a whole 2x2x1 slice. The times are simulated.
8 devices in a mesh: dp: 1 (over z), sp: 2 (over y), cp: 4 (over x, core).
Axes of the slice: x: 2, y: 2, z: 1, core: 2. Of those that a mesh axis runs over, the one named last changes fastest.
Arguments:
- x_chunk: bfloat16 [4096, 3072], P(('dp', 'sp', 'cp'))
- k_cache: bfloat16 [4096, 8, 128], P(('dp', 'sp', 'cp'))
- v_cache: bfloat16 [4096, 8, 128], P(('dp', 'sp', 'cp'))
- w_q: bfloat16 [3072, 3072], replicated
- w_k: bfloat16 [3072, 1024], replicated
- w_v: bfloat16 [3072, 1024], replicated
- w_o: bfloat16 [3072, 3072], replicated
Outputs:
- output 1: bfloat16 [4096, 3072], P(('dp', 'sp', 'cp'))
- output 2: bfloat16 [4096, 8, 128], P(('dp', 'sp', 'cp'))
- output 3: bfloat16 [4096, 8, 128], P(('dp', 'sp', 'cp'))
All inputs are finite; a program needn't handle non-finite values.
Results may differ from a plain program's by a relative error of at most 0.00496302.
Values are sent between devices in bfloat16 or wider.
A program may use at most 1 GiB of HBM per device.

v0:
```python
import jax
import jax.numpy as jnp
from jax import lax
from jax.sharding import PartitionSpec as P

ROPE_BASE = 500000
SEQ_AXES = ('sp', 'cp')


def rope_tables(positions, head_dim):
    inv_freq = 1.0 / (ROPE_BASE ** (jnp.arange(0, head_dim, 2, dtype=jnp.float32) / head_dim))
    angles = positions.astype(jnp.float32)[:, None] * inv_freq[None, :]
    return jnp.cos(angles), jnp.sin(angles)


def apply_rope(values, cos_t, sin_t):
    half_dim = values.shape[-1] // 2
    lo_half = values[..., :half_dim].astype(jnp.float32)
    hi_half = values[..., half_dim:].astype(jnp.float32)
    return jnp.concatenate([lo_half * cos_t - hi_half * sin_t, hi_half * cos_t + lo_half * sin_t], axis=-1).astype(jnp.bfloat16)


def attend_block(q_grp, keys, values, attn_scale, allowed=None):
    scores = jnp.einsum('qhgd,khd->hgqk', q_grp, keys, preferred_element_type=jnp.float32) * attn_scale
    if allowed is not None:
        scores = jnp.where(allowed, scores, -jnp.inf)
    row_max = jnp.max(scores, axis=-1)
    exp_scores = jnp.exp(scores - row_max[..., None])
    row_sum = jnp.sum(exp_scores, axis=-1)
    out_part = jnp.einsum('hgqk,khd->hgqd', exp_scores.astype(jnp.bfloat16), values, preferred_element_type=jnp.float32) / row_sum[..., None]
    return out_part, row_max + jnp.log(row_sum)


def merge_parts(out_a, lse_a, out_b, lse_b):
    lse_new = jnp.logaddexp(lse_a, lse_b)
    return out_a * jnp.exp(lse_a - lse_new)[..., None] + out_b * jnp.exp(lse_b - lse_new)[..., None], lse_new


def project_rows(x_loc, w_q, w_k, w_v, kv_heads, head_dim, positions):
    tok_loc = x_loc.shape[0]
    group_size = w_q.shape[1] // (kv_heads * head_dim)
    cos_t, sin_t = rope_tables(positions, head_dim)
    q_rows = jnp.dot(x_loc, w_q, preferred_element_type=jnp.float32).astype(jnp.bfloat16)
    q_grp = apply_rope(q_rows.reshape(tok_loc, kv_heads, group_size, head_dim), cos_t[:, None, None, :], sin_t[:, None, None, :])
    k_rows = jnp.dot(x_loc, w_k, preferred_element_type=jnp.float32).astype(jnp.bfloat16)
    k_new = apply_rope(k_rows.reshape(tok_loc, kv_heads, head_dim), cos_t[:, None, :], sin_t[:, None, :])
    v_new = jnp.dot(x_loc, w_v, preferred_element_type=jnp.float32).astype(jnp.bfloat16).reshape(tok_loc, kv_heads, head_dim)
    return q_grp, k_new, v_new


def solution(mesh):
    seq_size = mesh.shape['sp'] * mesh.shape['cp']
    cp_size = mesh.shape['cp']
    perm_next = [(src_idx, (src_idx + 1) % seq_size) for src_idx in range(seq_size)]
    row_spec = P(('dp', 'sp', 'cp'))

    def local_fn(x_loc, kc_loc, vc_loc, w_q, w_k, w_v, w_o):
        tok_loc, d_model = x_loc.shape
        cache_loc, kv_heads, head_dim = kc_loc.shape
        group_size = w_q.shape[1] // (kv_heads * head_dim)
        attn_scale = head_dim ** -0.5
        seq_idx = lax.axis_index('sp') * cp_size + lax.axis_index('cp')
        q_pos = seq_idx * tok_loc + jnp.arange(tok_loc)
        q_grp, k_new, v_new = project_rows(x_loc, w_q, w_k, w_v, kv_heads, head_dim, cache_loc * seq_size + q_pos)
        diag_mask = jnp.arange(tok_loc)[None, :] <= jnp.arange(tok_loc)[:, None]
        acc_out, acc_lse = attend_block(q_grp, k_new, v_new, attn_scale, diag_mask)
        k_fresh = lax.all_gather(k_new, SEQ_AXES, axis=0, tiled=True)
        v_fresh = lax.all_gather(v_new, SEQ_AXES, axis=0, tiled=True)

        def earlier_step(blk_idx, acc_state):
            k_blk = lax.dynamic_slice_in_dim(k_fresh, blk_idx * tok_loc, tok_loc, axis=0)
            v_blk = lax.dynamic_slice_in_dim(v_fresh, blk_idx * tok_loc, tok_loc, axis=0)
            out_part, lse_part = attend_block(q_grp, k_blk, v_blk, attn_scale)
            return merge_parts(acc_state[0], acc_state[1], out_part, lse_part)

        acc_out, acc_lse = lax.fori_loop(0, seq_idx, earlier_step, (acc_out, acc_lse))
        out_part, lse_part = attend_block(q_grp, kc_loc, vc_loc, attn_scale)
        acc_out, acc_lse = merge_parts(acc_out, acc_lse, out_part, lse_part)

        def cache_step(step_idx, loop_state):
            k_blk, v_blk, acc_o, acc_l = loop_state
            k_blk = lax.ppermute(k_blk, SEQ_AXES, perm_next)
            v_blk = lax.ppermute(v_blk, SEQ_AXES, perm_next)
            part_o, part_l = attend_block(q_grp, k_blk, v_blk, attn_scale)
            acc_o, acc_l = merge_parts(acc_o, acc_l, part_o, part_l)
            return k_blk, v_blk, acc_o, acc_l

        loop_state = lax.fori_loop(1, seq_size, cache_step, (kc_loc, vc_loc, acc_out, acc_lse))
        attn_bf = loop_state[2].astype(jnp.bfloat16)
        w_heads = w_o.reshape(kv_heads, group_size, head_dim, d_model)
        y_loc = jnp.einsum('hgqd,hgdm->qm', attn_bf, w_heads, preferred_element_type=jnp.float32).astype(jnp.bfloat16)
        return y_loc, k_new, v_new

    return jax.shard_map(local_fn, mesh=mesh, in_specs=(row_spec, row_spec, row_spec, P(), P(), P(), P()), out_specs=(row_spec, row_spec, row_spec), check_vma=False)
```

profile of v0, /device:TPU:0, one launch (start us, length us, event | category | flops | bytes accessed | tf_op | source)
XLA Modules:
  0.0 854.6 jit_solution(7148126038362881069)
XLA Ops:
  29.7 15.0 %convolution_convert_fusion = bf16[512,3072]{1,0:T(8,128)(2,1)} fusion(bf16[512,3072]{1,0:T(8,128)(2,1)S(1)} %copy-done, bf16[3072,3072]{1,0:T(8,128)(2,1)} %param.14), kind=kOutput, calls=%fused_computation.67 | convolution fusion | flops 9665249280 | bytes 25165824 | tf_op jit(solution)/shard_map/dot_general | solution.py:43
  77.2 11.2 %fusion.28 = f32[8,3,512]{2,1,0:T(4,128)S(1)} fusion(f32[8,512,512,3]{2,1,3,0:T(8,128)} %get-tuple-element.172, f32[8,3,512]{2,1,0:T(4,128)S(1)} %get-tuple-element.171, pred[512,512]{0,1:T(8,128)(4,1)S(1)} %iota_compare_fusion), kind=kLoop, calls=%fused_computation.42 | loop fusion | flops 25153536 | bytes 25526272 | tf_op jit(solution)/shard_map/reduce_sum | solution.py:29
  98.7 11.2 %fusion.31 = f32[8,3,512]{2,1,0:T(4,128)} fusion(f32[8,512,3,512]{1,3,2,0:T(8,128)} %get-tuple-element.174, f32[8,3,512]{2,1,0:T(4,128)S(1)} %get-tuple-element.173), kind=kLoop, calls=%fused_computation.45 | loop fusion | flops 18862080 | bytes 25264128 | tf_op jit(solution)/shard_map/reduce_sum | solution.py:29
  109.9 14.2 %broadcast_divide_fusion = f32[8,3,512,128]{3,2,1,0:T(8,128)} fusion(f32[8,3,512]{2,1,0:T(4,128)S(1)} %fusion.28, f32[8,512,512,3]{2,1,3,0:T(8,128)} %get-tuple-element.172, f32[8,3,512]{2,1,0:T(4,128)S(1)} %get-tuple-element.171, pred[512,512]{0,1:T(8,128)(4,1)S(1)} %iota_compare_fusion, bf16[512,8,128,1]{2,1,0,3:T(8,128)(2,1)S(1)} %bitcast.133), kind=kOutput, calls=%fused_computation.70 | convolution fusion | flops 1637351424 | bytes 32866304 | tf_op jit(solution)/shard_map/hgqk,khd->hgqd/dot_general | solution.py:30
  125.2 16.8 %multiply_add_fusion.2 = f32[8,3,512,128]{3,2,1,0:T(8,128)} fusion(f32[8,3,512,128]{3,2,1,0:T(8,128)} %get-tuple-element.74, f32[8,3,512]{2,1,0:T(4,128)S(1)} %subtract_exponential_fusion.5, f32[8,3,512]{2,1,0:T(4,128)S(1)} %copy-done.10, f32[8,3,512]{2,1,0:T(4,128)S(1)} %get-tuple-element.155, f32[8,512,3,512]{1,3,2,0:T(8,128)} %get-tuple-element.174, ...), kind=kOutput, calls=%fused_computation.66 | convolution fusion | flops 1635778560 | bytes 38993920 | tf_op jit(solution)/shard_map/hgqk,khd->hgqd/dot_general | solution.py:30
  142.0 689.7 %while.29 = (s32[]{:T(128)}, bf16[512,8,128]{2,0,1:T(8,128)(2,1)}, bf16[512,8,128]{2,0,1:T(8,128)(2,1)}, f32[8,3,512,128]{3,2,1,0:T(8,128)}, f32[8,3,512]{2,1,0:...) while((s32[]{:T(128)}, bf16[512,8,128]{2,0,1:T(8,128)(2,1)}, ...), condition=%wide.region_11.12_spmd, body=%wide.region_8.11_spmd.sunk | while | flops 3277971456 | bytes 257687824 | solution.py:88
  142.0 40.4 %collective-permute-start = (bf16[512,8,128]{2,0,1:T(8,128)(2,1)}, bf16[512,8,128]{2,0,1:T(8,128)(2,1)}, u32[]{:S(2)}, u32[]{:S(2)}) collective-permute-start(bf16[512,8,128]{2,0,1:T(8,128)(2,1)} %get-tuple-element.313), channel_id=1, source_target_pairs={{0,1},{1,2},{2,3},{3,4},{4,5},{5,6},{6,7},{7,0}} | collective-permute-start | bytes 3145736 | tf_op jit(solution)/shard_map/while/body/eval_jaxpr/ppermute | solution.py:82
  182.4 43.0 %collective-permute-start.1 = (bf16[512,8,128]{2,0,1:T(8,128)(2,1)}, bf16[512,8,128]{2,0,1:T(8,128)(2,1)}, u32[]{:S(2)}, u32[]{:S(2)}) collective-permute-start(bf16[512,8,128]{2,0,1:T(8,128)(2,1)} %get-tuple-element.314), channel_id=1, source_target_pairs={{0,1},{1,2},{2,3},{3,4},{4,5},{5,6},{6,7},{7,0}} | collective-permute-start | bytes 3145736 | tf_op jit(solution)/shard_map/while/body/eval_jaxpr/ppermute | solution.py:83
  225.3 214.6 %collective-permute-done = bf16[512,8,128]{2,0,1:T(8,128)(2,1)} collective-permute-done((bf16[512,8,128]{2,0,1:T(8,128)(2,1)}, bf16[512,8,128]{2,0,1:T(8,128)(2,1)}, u32[]{:S(2)}, u32[]{:S(2)}) %collective-permute-start) | collective-permute-done | bytes 1048608 | tf_op jit(solution)/shard_map/while/body/eval_jaxpr/ppermute | solution.py:82
  439.9 11.6 %bitcast_reduce_fusion.6 = (f32[8,3,512]{2,1,0:T(4,128)S(1)}, f32[8,512,512,3]{2,1,3,0:T(8,128)}) fusion(bf16[512,8,3,128]{3,0,2,1:T(8,128)(2,1)S(1)} %get-tuple-element.324, bf16[512,8,128]{2,0,1:T(8,128)(2,1)} %collective-permute-done), kind=kOutput, calls=%fused_computation.21.clone.1 | convolution fusion | flops 1623183360 | bytes 29409280 | tf_op jit(solution)/shard_map/while/body/eval_jaxpr/qhgd,khd->hgqk/dot_general | solution.py:24
  451.5 10.7 %fusion.97 = f32[8,3,512]{2,1,0:T(4,128)S(1)} fusion(f32[8,512,512,3]{2,1,3,0:T(8,128)} %get-tuple-element.269, f32[8,3,512]{2,1,0:T(4,128)S(1)} %get-tuple-element.268), kind=kLoop, calls=%fused_computation.24.clone.1 | loop fusion | flops 18862080 | bytes 25264128 | tf_op jit(solution)/shard_map/while/body/eval_jaxpr/reduce_sum | solution.py:29
  468.5 11.7 %multiply_add_fusion.6 = f32[8,3,512,128]{3,2,1,0:T(8,128)S(1)} fusion(f32[8,3,512,128]{3,2,1,0:T(8,128)S(1)} %copy-done.11, f32[8,3,512]{2,1,0:T(4,128)S(1)} %subtract_exponential_fusion.14, f32[8,3,512]{2,1,0:T(4,128)S(1)} %fusion.97, f32[8,3,512]{2,1,0:T(4,128)S(1)} %get-tuple-element.271, f32[8,512,512,3]{2,1,3,0:T(8,128)S(1)} %copy-done.2, ...), kind=kOutput, calls=%fused_computation.28.clone.1 | convolution fusion | flops 1635778560 | bytes 38993920 | tf_op jit(solution)/shard_map/while/body/eval_jaxpr/hgqk,khd->hgqd/dot_general | solution.py:30
  482.9 15.1 %collective-permute-done = bf16[512,8,128]{2,0,1:T(8,128)(2,1)} collective-permute-done((bf16[512,8,128]{2,0,1:T(8,128)(2,1)}, bf16[512,8,128]{2,0,1:T(8,128)(2,1)}, u32[]{:S(2)}, u32[]{:S(2)}) %collective-permute-start) | collective-permute-done | bytes 1048608 | tf_op jit(solution)/shard_map/while/body/eval_jaxpr/ppermute | solution.py:82
  498.0 11.6 %bitcast_reduce_fusion.6 = (f32[8,3,512]{2,1,0:T(4,128)S(1)}, f32[8,512,512,3]{2,1,3,0:T(8,128)}) fusion(bf16[512,8,3,128]{3,0,2,1:T(8,128)(2,1)S(1)} %get-tuple-element.324, bf16[512,8,128]{2,0,1:T(8,128)(2,1)} %collective-permute-done), kind=kOutput, calls=%fused_computation.21.clone.1 | convolution fusion | flops 1623183360 | bytes 29409280 | tf_op jit(solution)/shard_map/while/body/eval_jaxpr/qhgd,khd->hgqk/dot_general | solution.py:24
  509.6 10.7 %fusion.97 = f32[8,3,512]{2,1,0:T(4,128)S(1)} fusion(f32[8,512,512,3]{2,1,3,0:T(8,128)} %get-tuple-element.269, f32[8,3,512]{2,1,0:T(4,128)S(1)} %get-tuple-element.268), kind=kLoop, calls=%fused_computation.24.clone.1 | loop fusion | flops 18862080 | bytes 25264128 | tf_op jit(solution)/shard_map/while/body/eval_jaxpr/reduce_sum | solution.py:29
  526.7 11.7 %multiply_add_fusion.6 = f32[8,3,512,128]{3,2,1,0:T(8,128)S(1)} fusion(f32[8,3,512,128]{3,2,1,0:T(8,128)S(1)} %copy-done.11, f32[8,3,512]{2,1,0:T(4,128)S(1)} %subtract_exponential_fusion.14, f32[8,3,512]{2,1,0:T(4,128)S(1)} %fusion.97, f32[8,3,512]{2,1,0:T(4,128)S(1)} %get-tuple-element.271, f32[8,512,512,3]{2,1,3,0:T(8,128)S(1)} %copy-done.2, ...), kind=kOutput, calls=%fused_computation.28.clone.1 | convolution fusion | flops 1635778560 | bytes 38993920 | tf_op jit(solution)/shard_map/while/body/eval_jaxpr/hgqk,khd->hgqd/dot_general | solution.py:30
  541.0 15.1 %collective-permute-done = bf16[512,8,128]{2,0,1:T(8,128)(2,1)} collective-permute-done((bf16[512,8,128]{2,0,1:T(8,128)(2,1)}, bf16[512,8,128]{2,0,1:T(8,128)(2,1)}, u32[]{:S(2)}, u32[]{:S(2)}) %collective-permute-start) | collective-permute-done | bytes 1048608 | tf_op jit(solution)/shard_map/while/body/eval_jaxpr/ppermute | solution.py:82
  556.2 11.6 %bitcast_reduce_fusion.6 = (f32[8,3,512]{2,1,0:T(4,128)S(1)}, f32[8,512,512,3]{2,1,3,0:T(8,128)}) fusion(bf16[512,8,3,128]{3,0,2,1:T(8,128)(2,1)S(1)} %get-tuple-element.324, bf16[512,8,128]{2,0,1:T(8,128)(2,1)} %collective-permute-done), kind=kOutput, calls=%fused_computation.21.clone.1 | convolution fusion | flops 1623183360 | bytes 29409280 | tf_op jit(solution)/shard_map/while/body/eval_jaxpr/qhgd,khd->hgqk/dot_general | solution.py:24
  584.8 11.7 %multiply_add_fusion.6 = f32[8,3,512,128]{3,2,1,0:T(8,128)S(1)} fusion(f32[8,3,512,128]{3,2,1,0:T(8,128)S(1)} %copy-done.11, f32[8,3,512]{2,1,0:T(4,128)S(1)} %subtract_exponential_fusion.14, f32[8,3,512]{2,1,0:T(4,128)S(1)} %fusion.97, f32[8,3,512]{2,1,0:T(4,128)S(1)} %get-tuple-element.271, f32[8,512,512,3]{2,1,3,0:T(8,128)S(1)} %copy-done.2, ...), kind=kOutput, calls=%fused_computation.28.clone.1 | convolution fusion | flops 1635778560 | bytes 38993920 | tf_op jit(solution)/shard_map/while/body/eval_jaxpr/hgqk,khd->hgqd/dot_general | solution.py:30
  599.2 15.1 %collective-permute-done = bf16[512,8,128]{2,0,1:T(8,128)(2,1)} collective-permute-done((bf16[512,8,128]{2,0,1:T(8,128)(2,1)}, bf16[512,8,128]{2,0,1:T(8,128)(2,1)}, u32[]{:S(2)}, u32[]{:S(2)}) %collective-permute-start) | collective-permute-done | bytes 1048608 | tf_op jit(solution)/shard_map/while/body/eval_jaxpr/ppermute | solution.py:82
  614.3 11.6 %bitcast_reduce_fusion.6 = (f32[8,3,512]{2,1,0:T(4,128)S(1)}, f32[8,512,512,3]{2,1,3,0:T(8,128)}) fusion(bf16[512,8,3,128]{3,0,2,1:T(8,128)(2,1)S(1)} %get-tuple-element.324, bf16[512,8,128]{2,0,1:T(8,128)(2,1)} %collective-permute-done), kind=kOutput, calls=%fused_computation.21.clone.1 | convolution fusion | flops 1623183360 | bytes 29409280 | tf_op jit(solution)/shard_map/while/body/eval_jaxpr/qhgd,khd->hgqk/dot_general | solution.py:24
  642.9 11.7 %multiply_add_fusion.6 = f32[8,3,512,128]{3,2,1,0:T(8,128)S(1)} fusion(f32[8,3,512,128]{3,2,1,0:T(8,128)S(1)} %copy-done.11, f32[8,3,512]{2,1,0:T(4,128)S(1)} %subtract_exponential_fusion.14, f32[8,3,512]{2,1,0:T(4,128)S(1)} %fusion.97, f32[8,3,512]{2,1,0:T(4,128)S(1)} %get-tuple-element.271, f32[8,512,512,3]{2,1,3,0:T(8,128)S(1)} %copy-done.2, ...), kind=kOutput, calls=%fused_computation.28.clone.1 | convolution fusion | flops 1635778560 | bytes 38993920 | tf_op jit(solution)/shard_map/while/body/eval_jaxpr/hgqk,khd->hgqd/dot_general | solution.py:30
  657.3 15.1 %collective-permute-done = bf16[512,8,128]{2,0,1:T(8,128)(2,1)} collective-permute-done((bf16[512,8,128]{2,0,1:T(8,128)(2,1)}, bf16[512,8,128]{2,0,1:T(8,128)(2,1)}, u32[]{:S(2)}, u32[]{:S(2)}) %collective-permute-start) | collective-permute-done | bytes 1048608 | tf_op jit(solution)/shard_map/while/body/eval_jaxpr/ppermute | solution.py:82
  672.4 11.6 %bitcast_reduce_fusion.6 = (f32[8,3,512]{2,1,0:T(4,128)S(1)}, f32[8,512,512,3]{2,1,3,0:T(8,128)}) fusion(bf16[512,8,3,128]{3,0,2,1:T(8,128)(2,1)S(1)} %get-tuple-element.324, bf16[512,8,128]{2,0,1:T(8,128)(2,1)} %collective-permute-done), kind=kOutput, calls=%fused_computation.21.clone.1 | convolution fusion | flops 1623183360 | bytes 29409280 | tf_op jit(solution)/shard_map/while/body/eval_jaxpr/qhgd,khd->hgqk/dot_general | solution.py:24
  701.0 11.7 %multiply_add_fusion.6 = f32[8,3,512,128]{3,2,1,0:T(8,128)S(1)} fusion(f32[8,3,512,128]{3,2,1,0:T(8,128)S(1)} %copy-done.11, f32[8,3,512]{2,1,0:T(4,128)S(1)} %subtract_exponential_fusion.14, f32[8,3,512]{2,1,0:T(4,128)S(1)} %fusion.97, f32[8,3,512]{2,1,0:T(4,128)S(1)} %get-tuple-element.271, f32[8,512,512,3]{2,1,3,0:T(8,128)S(1)} %copy-done.2, ...), kind=kOutput, calls=%fused_computation.28.clone.1 | convolution fusion | flops 1635778560 | bytes 38993920 | tf_op jit(solution)/shard_map/while/body/eval_jaxpr/hgqk,khd->hgqd/dot_general | solution.py:30
  715.4 15.1 %collective-permute-done = bf16[512,8,128]{2,0,1:T(8,128)(2,1)} collective-permute-done((bf16[512,8,128]{2,0,1:T(8,128)(2,1)}, bf16[512,8,128]{2,0,1:T(8,128)(2,1)}, u32[]{:S(2)}, u32[]{:S(2)}) %collective-permute-start) | collective-permute-done | bytes 1048608 | tf_op jit(solution)/shard_map/while/body/eval_jaxpr/ppermute | solution.py:82
  730.5 11.6 %bitcast_reduce_fusion.6 = (f32[8,3,512]{2,1,0:T(4,128)S(1)}, f32[8,512,512,3]{2,1,3,0:T(8,128)}) fusion(bf16[512,8,3,128]{3,0,2,1:T(8,128)(2,1)S(1)} %get-tuple-element.324, bf16[512,8,128]{2,0,1:T(8,128)(2,1)} %collective-permute-done), kind=kOutput, calls=%fused_computation.21.clone.1 | convolution fusion | flops 1623183360 | bytes 29409280 | tf_op jit(solution)/shard_map/while/body/eval_jaxpr/qhgd,khd->hgqk/dot_general | solution.py:24
  759.2 11.7 %multiply_add_fusion.6 = f32[8,3,512,128]{3,2,1,0:T(8,128)S(1)} fusion(f32[8,3,512,128]{3,2,1,0:T(8,128)S(1)} %copy-done.11, f32[8,3,512]{2,1,0:T(4,128)S(1)} %subtract_exponential_fusion.14, f32[8,3,512]{2,1,0:T(4,128)S(1)} %fusion.97, f32[8,3,512]{2,1,0:T(4,128)S(1)} %get-tuple-element.271, f32[8,512,512,3]{2,1,3,0:T(8,128)S(1)} %copy-done.2, ...), kind=kOutput, calls=%fused_computation.28.clone.1 | convolution fusion | flops 1635778560 | bytes 38993920 | tf_op jit(solution)/shard_map/while/body/eval_jaxpr/hgqk,khd->hgqd/dot_general | solution.py:30
  773.5 15.1 %collective-permute-done = bf16[512,8,128]{2,0,1:T(8,128)(2,1)} collective-permute-done((bf16[512,8,128]{2,0,1:T(8,128)(2,1)}, bf16[512,8,128]{2,0,1:T(8,128)(2,1)}, u32[]{:S(2)}, u32[]{:S(2)}) %collective-permute-start) | collective-permute-done | bytes 1048608 | tf_op jit(solution)/shard_map/while/body/eval_jaxpr/ppermute | solution.py:82
  788.7 11.6 %bitcast_reduce_fusion.6 = (f32[8,3,512]{2,1,0:T(4,128)S(1)}, f32[8,512,512,3]{2,1,3,0:T(8,128)}) fusion(bf16[512,8,3,128]{3,0,2,1:T(8,128)(2,1)S(1)} %get-tuple-element.324, bf16[512,8,128]{2,0,1:T(8,128)(2,1)} %collective-permute-done), kind=kOutput, calls=%fused_computation.21.clone.1 | convolution fusion | flops 1623183360 | bytes 29409280 | tf_op jit(solution)/shard_map/while/body/eval_jaxpr/qhgd,khd->hgqk/dot_general | solution.py:24
  817.3 11.7 %multiply_add_fusion.6 = f32[8,3,512,128]{3,2,1,0:T(8,128)S(1)} fusion(f32[8,3,512,128]{3,2,1,0:T(8,128)S(1)} %copy-done.11, f32[8,3,512]{2,1,0:T(4,128)S(1)} %subtract_exponential_fusion.14, f32[8,3,512]{2,1,0:T(4,128)S(1)} %fusion.97, f32[8,3,512]{2,1,0:T(4,128)S(1)} %get-tuple-element.271, f32[8,512,512,3]{2,1,3,0:T(8,128)S(1)} %copy-done.2, ...), kind=kOutput, calls=%fused_computation.28.clone.1 | convolution fusion | flops 1635778560 | bytes 38993920 | tf_op jit(solution)/shard_map/while/body/eval_jaxpr/hgqk,khd->hgqd/dot_general | solution.py:30
  831.7 15.7 %bitcast_convert_fusion = bf16[512,3072]{1,0:T(8,128)(2,1)} fusion(bf16[8,3,128,3072]{3,2,1,0:T(8,128)(2,1)} %bitcast.135, f32[8,3,512,128]{3,2,1,0:T(8,128)} %get-tuple-element.76), kind=kOutput, calls=%fused_computation.65 | convolution fusion | flops 9666822144 | bytes 28311552 | tf_op jit(solution)/shard_map/hgqd,hgdm->qm/dot_general | solution.py:91
  (146 shorter events, 182.7 us)
Async XLA Ops:
  7.2 116.9 %all-gather.3.cloned.1.call-start = ((), (), s32[]{:S(2)}) async-start(), calls=%async_computation | async-start | bytes 9437184 | tf_op jit(solution)/shard_map/all_gather | solution.py:67
  19.3 104.8 %all-gather.5.cloned.1.call-start = ((), (), s32[]{:S(2)}) async-start(), calls=%async_computation.1 | async-start | bytes 9437184 | tf_op jit(solution)/shard_map/all_gather | solution.py:68
  77.2 11.2 %copy-start.5 = (bf16[512,8,128]{2,1,0:T(8,128)(2,1)S(1)}, bf16[512,8,128]{2,1,0:T(8,128)(2,1)}, u32[]{:S(2)}) copy-start(bf16[512,8,128]{2,1,0:T(8,128)(2,1)} %param.12) | copy-start | bytes 3145732
  142.0 297.9 %collective-permute-start = (bf16[512,8,128]{2,0,1:T(8,128)(2,1)}, bf16[512,8,128]{2,0,1:T(8,128)(2,1)}, u32[]{:S(2)}, u32[]{:S(2)}) collective-permute-start(bf16[512,8,128]{2,0,1:T(8,128)(2,1)} %get-tuple-element.313), channel_id=1, source_target_pairs={{0,1},{1,2},{2,3},{3,4},{4,5},{5,6},{6,7},{7,0}} | collective-permute-start | bytes 3145736 | tf_op jit(solution)/shard_map/while/body/eval_jaxpr/ppermute | solution.py:82
  182.4 283.1 %collective-permute-start.1 = (bf16[512,8,128]{2,0,1:T(8,128)(2,1)}, bf16[512,8,128]{2,0,1:T(8,128)(2,1)}, u32[]{:S(2)}, u32[]{:S(2)}) collective-permute-start(bf16[512,8,128]{2,0,1:T(8,128)(2,1)} %get-tuple-element.314), channel_id=1, source_target_pairs={{0,1},{1,2},{2,3},{3,4},{4,5},{5,6},{6,7},{7,0}} | collective-permute-start | bytes 3145736 | tf_op jit(solution)/shard_map/while/body/eval_jaxpr/ppermute | solution.py:83
  439.9 28.6 %copy-start.11 = (f32[8,3,512,128]{3,2,1,0:T(8,128)S(1)}, f32[8,3,512,128]{3,2,1,0:T(8,128)}, u32[]{:S(2)}) copy-start(f32[8,3,512,128]{3,2,1,0:T(8,128)} %get-tuple-element.315) | copy-start | bytes 18874372 | tf_op jit(solution)/shard_map/while
  451.5 17.1 %copy-start.2 = (f32[8,512,512,3]{2,1,3,0:T(8,128)S(1)}, f32[8,512,512,3]{2,1,3,0:T(8,128)}, u32[]{:S(2)}) copy-start(f32[8,512,512,3]{2,1,3,0:T(8,128)} %get-tuple-element.269) | copy-start | bytes 75497472 | tf_op jit(solution)/shard_map/while
  482.9 15.1 %collective-permute-start = (bf16[512,8,128]{2,0,1:T(8,128)(2,1)}, bf16[512,8,128]{2,0,1:T(8,128)(2,1)}, u32[]{:S(2)}, u32[]{:S(2)}) collective-permute-start(bf16[512,8,128]{2,0,1:T(8,128)(2,1)} %get-tuple-element.313), channel_id=1, source_target_pairs={{0,1},{1,2},{2,3},{3,4},{4,5},{5,6},{6,7},{7,0}} | collective-permute-start | bytes 3145736 | tf_op jit(solution)/shard_map/while/body/eval_jaxpr/ppermute | solution.py:82
  482.9 40.7 %collective-permute-start.1 = (bf16[512,8,128]{2,0,1:T(8,128)(2,1)}, bf16[512,8,128]{2,0,1:T(8,128)(2,1)}, u32[]{:S(2)}, u32[]{:S(2)}) collective-permute-start(bf16[512,8,128]{2,0,1:T(8,128)(2,1)} %get-tuple-element.314), channel_id=1, source_target_pairs={{0,1},{1,2},{2,3},{3,4},{4,5},{5,6},{6,7},{7,0}} | collective-permute-start | bytes 3145736 | tf_op jit(solution)/shard_map/while/body/eval_jaxpr/ppermute | solution.py:83
  498.0 28.6 %copy-start.11 = (f32[8,3,512,128]{3,2,1,0:T(8,128)S(1)}, f32[8,3,512,128]{3,2,1,0:T(8,128)}, u32[]{:S(2)}) copy-start(f32[8,3,512,128]{3,2,1,0:T(8,128)} %get-tuple-element.315) | copy-start | bytes 18874372 | tf_op jit(solution)/shard_map/while
  509.6 17.1 %copy-start.2 = (f32[8,512,512,3]{2,1,3,0:T(8,128)S(1)}, f32[8,512,512,3]{2,1,3,0:T(8,128)}, u32[]{:S(2)}) copy-start(f32[8,512,512,3]{2,1,3,0:T(8,128)} %get-tuple-element.269) | copy-start | bytes 75497472 | tf_op jit(solution)/shard_map/while
  541.0 15.1 %collective-permute-start = (bf16[512,8,128]{2,0,1:T(8,128)(2,1)}, bf16[512,8,128]{2,0,1:T(8,128)(2,1)}, u32[]{:S(2)}, u32[]{:S(2)}) collective-permute-start(bf16[512,8,128]{2,0,1:T(8,128)(2,1)} %get-tuple-element.313), channel_id=1, source_target_pairs={{0,1},{1,2},{2,3},{3,4},{4,5},{5,6},{6,7},{7,0}} | collective-permute-start | bytes 3145736 | tf_op jit(solution)/shard_map/while/body/eval_jaxpr/ppermute | solution.py:82
  541.0 40.7 %collective-permute-start.1 = (bf16[512,8,128]{2,0,1:T(8,128)(2,1)}, bf16[512,8,128]{2,0,1:T(8,128)(2,1)}, u32[]{:S(2)}, u32[]{:S(2)}) collective-permute-start(bf16[512,8,128]{2,0,1:T(8,128)(2,1)} %get-tuple-element.314), channel_id=1, source_target_pairs={{0,1},{1,2},{2,3},{3,4},{4,5},{5,6},{6,7},{7,0}} | collective-permute-start | bytes 3145736 | tf_op jit(solution)/shard_map/while/body/eval_jaxpr/ppermute | solution.py:83
  556.2 28.6 %copy-start.11 = (f32[8,3,512,128]{3,2,1,0:T(8,128)S(1)}, f32[8,3,512,128]{3,2,1,0:T(8,128)}, u32[]{:S(2)}) copy-start(f32[8,3,512,128]{3,2,1,0:T(8,128)} %get-tuple-element.315) | copy-start | bytes 18874372 | tf_op jit(solution)/shard_map/while
  567.7 17.1 %copy-start.2 = (f32[8,512,512,3]{2,1,3,0:T(8,128)S(1)}, f32[8,512,512,3]{2,1,3,0:T(8,128)}, u32[]{:S(2)}) copy-start(f32[8,512,512,3]{2,1,3,0:T(8,128)} %get-tuple-element.269) | copy-start | bytes 75497472 | tf_op jit(solution)/shard_map/while
  599.2 15.1 %collective-permute-start = (bf16[512,8,128]{2,0,1:T(8,128)(2,1)}, bf16[512,8,128]{2,0,1:T(8,128)(2,1)}, u32[]{:S(2)}, u32[]{:S(2)}) collective-permute-start(bf16[512,8,128]{2,0,1:T(8,128)(2,1)} %get-tuple-element.313), channel_id=1, source_target_pairs={{0,1},{1,2},{2,3},{3,4},{4,5},{5,6},{6,7},{7,0}} | collective-permute-start | bytes 3145736 | tf_op jit(solution)/shard_map/while/body/eval_jaxpr/ppermute | solution.py:82
  599.2 40.7 %collective-permute-start.1 = (bf16[512,8,128]{2,0,1:T(8,128)(2,1)}, bf16[512,8,128]{2,0,1:T(8,128)(2,1)}, u32[]{:S(2)}, u32[]{:S(2)}) collective-permute-start(bf16[512,8,128]{2,0,1:T(8,128)(2,1)} %get-tuple-element.314), channel_id=1, source_target_pairs={{0,1},{1,2},{2,3},{3,4},{4,5},{5,6},{6,7},{7,0}} | collective-permute-start | bytes 3145736 | tf_op jit(solution)/shard_map/while/body/eval_jaxpr/ppermute | solution.py:83
  614.3 28.6 %copy-start.11 = (f32[8,3,512,128]{3,2,1,0:T(8,128)S(1)}, f32[8,3,512,128]{3,2,1,0:T(8,128)}, u32[]{:S(2)}) copy-start(f32[8,3,512,128]{3,2,1,0:T(8,128)} %get-tuple-element.315) | copy-start | bytes 18874372 | tf_op jit(solution)/shard_map/while
  625.8 17.1 %copy-start.2 = (f32[8,512,512,3]{2,1,3,0:T(8,128)S(1)}, f32[8,512,512,3]{2,1,3,0:T(8,128)}, u32[]{:S(2)}) copy-start(f32[8,512,512,3]{2,1,3,0:T(8,128)} %get-tuple-element.269) | copy-start | bytes 75497472 | tf_op jit(solution)/shard_map/while
  657.3 15.1 %collective-permute-start = (bf16[512,8,128]{2,0,1:T(8,128)(2,1)}, bf16[512,8,128]{2,0,1:T(8,128)(2,1)}, u32[]{:S(2)}, u32[]{:S(2)}) collective-permute-start(bf16[512,8,128]{2,0,1:T(8,128)(2,1)} %get-tuple-element.313), channel_id=1, source_target_pairs={{0,1},{1,2},{2,3},{3,4},{4,5},{5,6},{6,7},{7,0}} | collective-permute-start | bytes 3145736 | tf_op jit(solution)/shard_map/while/body/eval_jaxpr/ppermute | solution.py:82
  657.3 40.7 %collective-permute-start.1 = (bf16[512,8,128]{2,0,1:T(8,128)(2,1)}, bf16[512,8,128]{2,0,1:T(8,128)(2,1)}, u32[]{:S(2)}, u32[]{:S(2)}) collective-permute-start(bf16[512,8,128]{2,0,1:T(8,128)(2,1)} %get-tuple-element.314), channel_id=1, source_target_pairs={{0,1},{1,2},{2,3},{3,4},{4,5},{5,6},{6,7},{7,0}} | collective-permute-start | bytes 3145736 | tf_op jit(solution)/shard_map/while/body/eval_jaxpr/ppermute | solution.py:83
  672.4 28.6 %copy-start.11 = (f32[8,3,512,128]{3,2,1,0:T(8,128)S(1)}, f32[8,3,512,128]{3,2,1,0:T(8,128)}, u32[]{:S(2)}) copy-start(f32[8,3,512,128]{3,2,1,0:T(8,128)} %get-tuple-element.315) | copy-start | bytes 18874372 | tf_op jit(solution)/shard_map/while
  684.0 17.1 %copy-start.2 = (f32[8,512,512,3]{2,1,3,0:T(8,128)S(1)}, f32[8,512,512,3]{2,1,3,0:T(8,128)}, u32[]{:S(2)}) copy-start(f32[8,512,512,3]{2,1,3,0:T(8,128)} %get-tuple-element.269) | copy-start | bytes 75497472 | tf_op jit(solution)/shard_map/while
  715.4 15.1 %collective-permute-start = (bf16[512,8,128]{2,0,1:T(8,128)(2,1)}, bf16[512,8,128]{2,0,1:T(8,128)(2,1)}, u32[]{:S(2)}, u32[]{:S(2)}) collective-permute-start(bf16[512,8,128]{2,0,1:T(8,128)(2,1)} %get-tuple-element.313), channel_id=1, source_target_pairs={{0,1},{1,2},{2,3},{3,4},{4,5},{5,6},{6,7},{7,0}} | collective-permute-start | bytes 3145736 | tf_op jit(solution)/shard_map/while/body/eval_jaxpr/ppermute | solution.py:82
  715.4 40.7 %collective-permute-start.1 = (bf16[512,8,128]{2,0,1:T(8,128)(2,1)}, bf16[512,8,128]{2,0,1:T(8,128)(2,1)}, u32[]{:S(2)}, u32[]{:S(2)}) collective-permute-start(bf16[512,8,128]{2,0,1:T(8,128)(2,1)} %get-tuple-element.314), channel_id=1, source_target_pairs={{0,1},{1,2},{2,3},{3,4},{4,5},{5,6},{6,7},{7,0}} | collective-permute-start | bytes 3145736 | tf_op jit(solution)/shard_map/while/body/eval_jaxpr/ppermute | solution.py:83
  730.5 28.6 %copy-start.11 = (f32[8,3,512,128]{3,2,1,0:T(8,128)S(1)}, f32[8,3,512,128]{3,2,1,0:T(8,128)}, u32[]{:S(2)}) copy-start(f32[8,3,512,128]{3,2,1,0:T(8,128)} %get-tuple-element.315) | copy-start | bytes 18874372 | tf_op jit(solution)/shard_map/while
  742.1 17.1 %copy-start.2 = (f32[8,512,512,3]{2,1,3,0:T(8,128)S(1)}, f32[8,512,512,3]{2,1,3,0:T(8,128)}, u32[]{:S(2)}) copy-start(f32[8,512,512,3]{2,1,3,0:T(8,128)} %get-tuple-element.269) | copy-start | bytes 75497472 | tf_op jit(solution)/shard_map/while
  773.5 15.1 %collective-permute-start = (bf16[512,8,128]{2,0,1:T(8,128)(2,1)}, bf16[512,8,128]{2,0,1:T(8,128)(2,1)}, u32[]{:S(2)}, u32[]{:S(2)}) collective-permute-start(bf16[512,8,128]{2,0,1:T(8,128)(2,1)} %get-tuple-element.313), channel_id=1, source_target_pairs={{0,1},{1,2},{2,3},{3,4},{4,5},{5,6},{6,7},{7,0}} | collective-permute-start | bytes 3145736 | tf_op jit(solution)/shard_map/while/body/eval_jaxpr/ppermute | solution.py:82
  773.5 40.7 %collective-permute-start.1 = (bf16[512,8,128]{2,0,1:T(8,128)(2,1)}, bf16[512,8,128]{2,0,1:T(8,128)(2,1)}, u32[]{:S(2)}, u32[]{:S(2)}) collective-permute-start(bf16[512,8,128]{2,0,1:T(8,128)(2,1)} %get-tuple-element.314), channel_id=1, source_target_pairs={{0,1},{1,2},{2,3},{3,4},{4,5},{5,6},{6,7},{7,0}} | collective-permute-start | bytes 3145736 | tf_op jit(solution)/shard_map/while/body/eval_jaxpr/ppermute | solution.py:83
  788.7 28.6 %copy-start.11 = (f32[8,3,512,128]{3,2,1,0:T(8,128)S(1)}, f32[8,3,512,128]{3,2,1,0:T(8,128)}, u32[]{:S(2)}) copy-start(f32[8,3,512,128]{3,2,1,0:T(8,128)} %get-tuple-element.315) | copy-start | bytes 18874372 | tf_op jit(solution)/shard_map/while
  800.2 17.1 %copy-start.2 = (f32[8,512,512,3]{2,1,3,0:T(8,128)S(1)}, f32[8,512,512,3]{2,1,3,0:T(8,128)}, u32[]{:S(2)}) copy-start(f32[8,512,512,3]{2,1,3,0:T(8,128)} %get-tuple-element.269) | copy-start | bytes 75497472 | tf_op jit(solution)/shard_map/while
  831.7 15.7 %copy-start.1 = (bf16[512,3072]{1,0:T(8,128)(2,1)S(1)}, bf16[512,3072]{1,0:T(8,128)(2,1)}, u32[]{:S(2)}) copy-start(bf16[512,3072]{1,0:T(8,128)(2,1)} %param.11) | copy-start | bytes 9437188
  (15 other events, 52.3 us)
Sparse Core Ops, SparseCore 0:
  19.4 51.1 all-gather.2
  73.0 48.3 all-gather.4
where the time goes:
time: 863 us; the launch traced here: 855 us
  waiting for transfers between devices  305 us (35%)
  matrix products  257 us (30%)
  other arithmetic  107 us (12%)
  local copies, waits for them, and re-layouts  86.3 us (10%)
  starting transfers between devices  83.5 us (10%)
  between operations  14.7 us (2%)
    ppermute x7, waiting for transfers between devices, cache_step(): k_blk = lax.ppermute(k_blk, SEQ_AXES, perm_next)  305 us
    dot_general x9, matrix products, attend_block(): jnp.einsum('hgqk,khd->hgqd', exp_scores.astype(jnp.bfloat16), values, pre...  113 us
    dot_general x9, matrix products, attend_block(): jnp.einsum('qhgd,khd->hgqk', q_grp, keys, preferred_element_type=jnp.floa...  101 us
    reduce_sum x9, other arithmetic, attend_block(): row_sum = jnp.sum(exp_scores, axis=-1)  97.5 us
    while x56, local copies, waits for them, and re-layouts  61.6 us
    ppermute x7, starting transfers between devices, cache_step(): v_blk = lax.ppermute(v_blk, SEQ_AXES, perm_next)  43 us
    ppermute x7, starting transfers between devices, cache_step(): k_blk = lax.ppermute(k_blk, SEQ_AXES, perm_next)  40.4 us
  transfers between devices with their start and end apart: 16, of which 7 were waited for; matrix products, arithmetic and copies ran while one was open for 33% of the time, Pallas kernels for 0%

commit v1 on v0

v1 whole, which is shorter than its diff:
```python
import functools

import jax
import jax.numpy as jnp
from jax import lax
from jax.experimental import pallas as pl
from jax.experimental.pallas import tpu as pltpu
from jax.sharding import PartitionSpec as P

ROPE_BASE = 500000
MESH_ID = pl.DeviceIdType.MESH
NDEV = 8
NEG = -1e30
LOG2E = 1.4426950408889634
KC, VC, QN, KN, VN = range(5)


def rope_tables(positions, head_dim):
    inv_freq = 1.0 / (ROPE_BASE ** (jnp.arange(0, head_dim, 2, dtype=jnp.float32) / head_dim))
    angles = positions.astype(jnp.float32)[:, None] * inv_freq[None, :]
    return jnp.cos(angles), jnp.sin(angles)


def apply_rope(values, cos_t, sin_t):
    half_dim = values.shape[-1] // 2
    lo_half = values[..., :half_dim].astype(jnp.float32)
    hi_half = values[..., half_dim:].astype(jnp.float32)
    return jnp.concatenate([lo_half * cos_t - hi_half * sin_t, hi_half * cos_t + lo_half * sin_t], axis=-1).astype(jnp.bfloat16)


def attn_kernel(group, tok, scale, q_hbm, kn_hbm, vn_hbm, kc_hbm, vc_hbm, o_hbm,
                q_s, kc_s, vc_s, kn_s, vn_s, acc, m_s, l_s, s_s, osend, send_sem, recv_sem, osend_sem, orecv_sem):
    y = lax.axis_index('sp')
    xc = lax.axis_index('cp')
    x, c = xc // 2, xc % 2
    me = y * 4 + xc
    c2 = scale * LOG2E
    hd = 128
    gw = group * hd

    def peer(k):
        py, px, pc = (y + k // 4) % 2, (x + (k // 2) % 2) % 2, (c + k % 2) % 2
        return py * 4 + px * 2 + pc, (0, py, px * 2 + pc)

    barrier = pltpu.get_barrier_semaphore()
    for k in range(1, NDEV):
        pl.semaphore_signal(barrier, inc=1, device_id=peer(k)[1], device_id_type=MESH_ID)
    srcs = (kc_hbm, vc_hbm, q_hbm, kn_hbm, vn_hbm)
    dsts = (kc_s, vc_s, q_s, kn_s, vn_s)

    def local(kind):
        slot = me if kind in (KN, VN) else 0
        return pltpu.make_async_copy(srcs[kind].at[me], dsts[kind].at[slot], recv_sem.at[kind, 0])

    def remote(kind, k):
        p, did = peer(k)
        slot = me if kind in (KN, VN) else k
        return pltpu.make_async_remote_copy(src_ref=srcs[kind].at[p], dst_ref=dsts[kind].at[slot], send_sem=send_sem.at[kind, k],
                                            recv_sem=recv_sem.at[kind, k], device_id=did, device_id_type=MESH_ID)

    def arrived(kind, k):
        slot = peer(k)[0] if kind in (KN, VN) else k
        pltpu.make_async_copy(srcs[kind].at[0], dsts[kind].at[slot], recv_sem.at[kind, k]).wait()

    for kind in range(5):
        local(kind).start()
    acc[...] = jnp.zeros_like(acc)
    l_s[...] = jnp.zeros_like(l_s)
    m_s[...] = jnp.full(m_s.shape, NEG, jnp.float32)
    pl.semaphore_wait(barrier, NDEV - 1)
    order = (1, 2, 4, 6, 3, 5, 7)
    for kinds in ((KC, VC), (QN,), (KN, VN)):
        for k in order:
            for kind in kinds:
                remote(kind, k).start()

    def qk(keys, k, r):
        return lax.dot_general(keys, q_s[k, r * tok:(r + 1) * tok, :], (((1,), (1,)), ((), ())), preferred_element_type=jnp.float32)

    def soft_pv(k, r, s, mx, vt):
        cols = slice(r * tok, (r + 1) * tok)
        m_old = m_s[k, :, cols]
        m_new = jnp.maximum(m_old, mx * c2)
        m_s[k, :, cols] = m_new
        alpha = jnp.exp2(m_old - m_new)
        p = jnp.exp2(s * c2 - m_new)
        l_s[k, :, cols] = l_s[k, :, cols] * alpha + jnp.sum(p, axis=0, keepdims=True)
        pv = lax.dot_general(vt, p.astype(jnp.bfloat16), (((1,), (0,)), ((), ())), preferred_element_type=jnp.float32)
        acc[k, :, cols] = acc[k, :, cols] * alpha + pv

    def kchunk(j):
        return kc_s[pl.ds(2 * j, 2)].reshape(2 * tok, hd)

    def vpv(k, r, s, mx, j):
        vt = jnp.concatenate([vc_s[2 * j], vc_s[2 * j + 1]], axis=1)
        soft_pv(k, r, s, mx, vt)

    for kind, k in ((KC, 0), (KC, 1), (QN, 0), (VC, 0), (VC, 1)):
        arrived(kind, k)
    s0 = qk(kchunk(0), 0, 0)
    s_s[0] = s0
    n1 = NDEV * 4

    def phase1(t, mx):
        k, j = t // 4, t % 4
        tn = jnp.minimum(t + 1, n1 - 1)
        kn_, jn_ = tn // 4, tn % 4

        @pl.when(jnp.logical_and(k == 0, j < 3))
        def _():
            for kind in (KC, VC):
                arrived(kind, 2 * jn_)
                arrived(kind, 2 * jn_ + 1)

        @pl.when(jnp.logical_and(j == 3, k < NDEV - 1))
        def _():
            arrived(QN, kn_)

        for r in range(group):
            nr = (r + 1) % group
            s_next = qk(kchunk(j), k, nr) if nr else qk(kchunk(jn_), kn_, 0)
            cur = s_s[r]
            s_s[nr] = s_next
            vpv(k, r, cur, mx, j)
            mx = jnp.max(s_next, axis=0, keepdims=True)
        return mx

    lax.fori_loop(0, n1, phase1, jnp.max(s0, axis=0, keepdims=True))

    for k in range(NDEV):
        arrived(KN, k)
        arrived(VN, k)
    ahead = lax.broadcasted_iota(jnp.int32, (tok, tok), 0) <= lax.broadcasted_iota(jnp.int32, (tok, tok), 1)
    half = pl.ds(0, tok)

    def owner_cols(dev):
        return pl.ds(pl.multiple_of(dev * gw, gw), gw)

    def send_out(k):
        return pltpu.make_async_remote_copy(src_ref=osend.at[k], dst_ref=o_hbm.at[:, owner_cols(me)], send_sem=osend_sem.at[k],
                                            recv_sem=orecv_sem.at[k], device_id=peer(k)[1], device_id_type=MESH_ID)

    def phase2(kk, carry):
        k = NDEV - 1 - kk
        p = peer(k)[0]
        s = jnp.where(ahead, qk(kn_s[p], k, 0), NEG)
        s_s[0, half] = s
        mx = jnp.max(s, axis=0, keepdims=True)
        for r in range(group):
            nr = (r + 1) % group
            s_next = jnp.where(ahead, qk(kn_s[p], k, nr), NEG) if nr else qk(kn_s[0], k, 0)
            cur = s_s[r, half]
            s_s[nr, half] = s_next
            soft_pv(k, r, cur, mx, vn_s[p])
            mx = jnp.max(s_next, axis=0, keepdims=True)

        @pl.when(kk > 0)
        def _():
            send_out(k + 1).start()

        def earlier(j, mx):
            jn = jnp.minimum(j + 1, p - 1)
            for r in range(group):
                nr = (r + 1) % group
                s_next = qk(kn_s[j], k, nr) if nr else qk(kn_s[jn], k, 0)
                cur = s_s[r, half]
                s_s[nr, half] = s_next
                soft_pv(k, r, cur, mx, vn_s[j])
                mx = jnp.max(s_next, axis=0, keepdims=True)
            return mx

        lax.fori_loop(0, p, earlier, mx)
        for r in range(group):
            cols = slice(r * tok, (r + 1) * tok)
            o_t = acc[k, :, cols] * (1.0 / l_s[k, :, cols])
            osend[k, :, r * hd:(r + 1) * hd] = o_t.T.astype(jnp.bfloat16)
        return carry

    lax.fori_loop(0, NDEV, phase2, 0)
    own = pltpu.make_async_copy(osend.at[0], o_hbm.at[:, owner_cols(me)], orecv_sem.at[0])
    own.start()
    for k in range(1, NDEV):
        for kind in range(5):
            remote(kind, k).wait_send()
        send_out(k).wait_send()
        pltpu.make_async_copy(osend.at[k], o_hbm.at[:, owner_cols(peer(k)[0])], orecv_sem.at[k]).wait()
    own.wait()


def attention(q_t, kn_t, vn_t, kc_t, vc_t):
    kv_heads, rows, hd = q_t.shape
    tok = kn_t.shape[1]
    group = rows // tok
    bf, f32 = jnp.bfloat16, jnp.float32
    hbm = pl.BlockSpec(memory_space=pl.ANY)
    return pl.pallas_call(
        functools.partial(attn_kernel, group, tok, hd ** -0.5),
        out_shape=jax.ShapeDtypeStruct((tok, kv_heads * group * hd), bf),
        in_specs=[hbm] * 5,
        out_specs=hbm,
        scratch_shapes=[
            pltpu.VMEM((NDEV, rows, hd), bf),
            pltpu.VMEM((NDEV, tok, hd), bf),
            pltpu.VMEM((NDEV, hd, tok), bf),
            pltpu.VMEM((NDEV, tok, hd), bf),
            pltpu.VMEM((NDEV, hd, tok), bf),
            pltpu.VMEM((NDEV, hd, rows), f32),
            pltpu.VMEM((NDEV, 1, rows), f32),
            pltpu.VMEM((NDEV, 1, rows), f32),
            pltpu.VMEM((group, 2 * tok, tok), f32),
            pltpu.VMEM((NDEV, tok, group * hd), bf),
            pltpu.SemaphoreType.DMA((5, NDEV)),
            pltpu.SemaphoreType.DMA((5, NDEV)),
            pltpu.SemaphoreType.DMA((NDEV,)),
            pltpu.SemaphoreType.DMA((NDEV,)),
        ],
        compiler_params=pltpu.CompilerParams(collective_id=0, has_side_effects=True, vmem_limit_bytes=56 * 2**20),
        name='head_attention',
    )(q_t, kn_t, vn_t, kc_t, vc_t)


def solution(mesh):
    seq_size = mesh.shape['sp'] * mesh.shape['cp']
    cp_size = mesh.shape['cp']
    row_spec = P(('dp', 'sp', 'cp'))

    def local_fn(x_loc, kc_loc, vc_loc, w_q, w_k, w_v, w_o):
        tok, d_model = x_loc.shape
        cache_loc, kv_heads, hd = kc_loc.shape
        group = w_q.shape[1] // (kv_heads * hd)
        seq_idx = lax.axis_index('sp') * cp_size + lax.axis_index('cp')
        kc_t = jnp.transpose(kc_loc, (1, 0, 2))
        vc_t = jnp.transpose(vc_loc, (1, 2, 0))
        cos_t, sin_t = rope_tables(cache_loc * seq_size + seq_idx * tok + jnp.arange(tok), hd)
        k_rows = jnp.dot(x_loc, w_k, preferred_element_type=jnp.float32).astype(jnp.bfloat16)
        k_new = apply_rope(k_rows.reshape(tok, kv_heads, hd), cos_t[:, None, :], sin_t[:, None, :])
        v_new = jnp.dot(x_loc, w_v, preferred_element_type=jnp.float32).astype(jnp.bfloat16).reshape(tok, kv_heads, hd)
        q_rows = jnp.dot(x_loc, w_q, preferred_element_type=jnp.float32).astype(jnp.bfloat16)
        q_t = jnp.transpose(q_rows.reshape(tok, kv_heads, group, hd), (1, 2, 0, 3))
        q_t = apply_rope(q_t, cos_t, sin_t).reshape(kv_heads, group * tok, hd)
        o_rows = attention(q_t, jnp.transpose(k_new, (1, 0, 2)), jnp.transpose(v_new, (1, 2, 0)), kc_t, vc_t)
        y_loc = jnp.dot(o_rows, w_o, preferred_element_type=jnp.float32).astype(jnp.bfloat16)
        return y_loc, k_new, v_new

    return jax.shard_map(local_fn, mesh=mesh, in_specs=(row_spec, row_spec, row_spec, P(), P(), P(), P()), out_specs=(row_spec, row_spec, row_spec), check_vma=False)
```

time: 863 us -> 242 us (0.28)
  waiting for transfers between devices: 305 us -> 0 us
  matrix products: 257 us -> 45.2 us
  Pallas kernels: 0 us -> 145 us
  other arithmetic: 107 us -> 16 us
  starting transfers between devices: 83.5 us -> 0 us
  local copies, waits for them, and re-layouts: 86.3 us -> 35.2 us
  between operations: 14.7 us -> 0.73 us
    ppermute x14 -> x0, waiting for transfers between devices: 305 us -> none  [the longest x7 305 us: cache_step(): k_blk = lax.ppermute(k_blk, SEQ_AXES, perm_next)]
    dot_general x22 -> x4, matrix products: 257 us -> 45.2 us  [the longest x1 16 us: local_fn(): jnp.dot(o_rows, w_o, preferred_element_type=jnp.float32)]
    pallas_call x0 -> x1, Pallas kernels: none -> 145 us  [attention(): pl.pallas_call(functools.partial(attn_kernel, group, tok, hd ** (-0.5)),...]
    reduce_sum x9 -> x0, other arithmetic: 97.5 us -> none  [attend_block(): row_sum = jnp.sum(exp_scores, axis=-1)]
    ppermute x14 -> x0, starting transfers between devices: 83.4 us -> none  [the longest x7 43 us: cache_step(): v_blk = lax.ppermute(v_blk, SEQ_AXES, perm_next)]
    while x58 -> x0, local copies, waits for them, and re-layouts: 66.5 us -> none
  transfers between devices with their start and end apart: 16 -> 0, of which waited for: 7 -> 0; matrix products, arithmetic and copies ran while one was open for 33% -> 0% of each run, Pallas kernels for 0% -> 0%
where the time goes in v1:
time: 242 us
  Pallas kernels  145 us (60%)
  matrix products  45.2 us (19%)
  local copies, waits for them, and re-layouts  35.2 us (15%)
  other arithmetic  16 us (7%)
    pallas_call x1, Pallas kernels, attention(): pl.pallas_call(functools.partial(attn_kernel, group, tok, hd ** (-0.5)),...  145 us
    dot_general x1, matrix products, local_fn(): jnp.dot(o_rows, w_o, preferred_element_type=jnp.float32)  16 us
    dot_general x1, matrix products, local_fn(): jnp.dot(x_loc, w_q, preferred_element_type=jnp.float32).astype(jnp.bfloat16)  14.9 us
    unnamed x20, local copies, waits for them, and re-layouts  13.7 us
    another operation x2, local copies, waits for them, and re-layouts  8.32 us
    dot_general x1, matrix products, local_fn(): jnp.dot(x_loc, w_k, preferred_element_type=jnp.float32).astype(jnp.bfloat16)  7.16 us
    dot_general x1, matrix products, local_fn(): jnp.dot(x_loc, w_v, preferred_element_type=jnp.float32).astype(jnp.bfloat16)  7.16 us
    another operation x2, other arithmetic  7.08 us

profile of v1, /device:TPU:0, one launch (start us, length us, event | category | flops | bytes accessed | tf_op | source)
XLA Modules:
  0.0 241.8 jit_solution(9493838215790456147)
XLA Ops:
  0.6 0.0 copy-start
  0.7 0.5 multiply_cosine_fusion
  1.2 0.8 copy.34
  2.1 0.8 copy.36
  2.9 0.0 copy-done
  2.9 7.2 %convolution_convert_fusion.3 = bf16[512,1024]{1,0:T(8,128)(2,1)} fusion(bf16[512,3072]{1,0:T(8,128)(2,1)S(1)} %copy-done, bf16[3072,1024]{1,0:T(8,128)(2,1)} %param.11), kind=kOutput, calls=%fused_computation.20 | convolution fusion | flops 3221749760 | bytes 10485760 | tf_op jit(solution)/shard_map/dot_general | solution.py:235
  10.1 2.3 copy.32
  12.3 2.2 fusion.8
  14.6 2.4 copy.42
  16.9 2.4 copy.43
  19.3 2.3 fusion.5
  21.6 0.0 copy-start.2
  21.7 0.0 copy-start.4
  21.7 1.0 copy-done.2
  22.7 0.3 copy-done.4
  22.9 1.5 fusion.17.kn_hbm
  24.5 14.9 %convolution_convert_fusion.1 = bf16[512,3072]{1,0:T(8,128)(2,1)} fusion(bf16[512,3072]{1,0:T(8,128)(2,1)S(1)} %copy-done, bf16[3072,3072]{1,0:T(8,128)(2,1)} %param.10), kind=kOutput, calls=%fused_computation.1 | convolution fusion | flops 9665249280 | bytes 25165824 | tf_op jit(solution)/shard_map/dot_general | solution.py:238
  39.4 4.6 %copy.29 = bf16[512,3072]{0,1:T(8,128)(2,1)} copy(bf16[512,3072]{1,0:T(8,128)(2,1)} %convolution_convert_fusion.1) | data formatting | bytes 6291456 | tf_op jit(solution)/shard_map/convert_element_type | solution.py:238
  44.0 4.7 %fusion.1 = (bf16[8,3,512,64]{2,3,1,0:T(8,128)(2,1)}, bf16[8,3,512,64]{2,3,1,0:T(8,128)(2,1)}) fusion(f32[512,64]{0,1:T(8,128)S(1)} %get-tuple-element.19, f32[512,64]{0,1:T(8,128)S(1)} %get-tuple-element.18, bf16[8,3,512,128]{2,3,1,0:T(8,128)(2,1)} %bitcast.23), kind=kLoop, calls=%fused_computation.7 | loop fusion | flops 7864320 | bytes 6553600 | tf_op jit(solution)/shard_map/convert.5
  48.8 4.2 %copy.30 = bf16[8,3,512,64]{3,2,1,0:T(8,128)(2,1)} copy(bf16[8,3,512,64]{2,3,1,0:T(8,128)(2,1)} %get-tuple-element.12) | data formatting | bytes 3145728 | tf_op jit(solution)/shard_map/convert.5
  53.0 4.1 %copy.31 = bf16[8,3,512,64]{3,2,1,0:T(8,128)(2,1)} copy(bf16[8,3,512,64]{2,3,1,0:T(8,128)(2,1)} %get-tuple-element.13) | data formatting | bytes 3145728 | tf_op jit(solution)/shard_map/convert.4
  57.1 6.2 %pad_maximum_fusion.q_hbm = bf16[8,1536,128]{2,1,0:T(8,128)(2,1)} fusion(bf16[8,1536,64]{2,1,0:T(8,128)(2,1)} %bitcast.25, bf16[8,1536,64]{2,1,0:T(8,128)(2,1)} %bitcast.24), kind=kLoop, calls=%fused_computation.10 | loop fusion | flops 6291456 | bytes 6291456 | tf_op jit(solution)/shard_map/concatenate | solution.py:28
  63.3 7.2 %convolution_convert_fusion.2 = bf16[512,1024]{1,0:T(8,128)(2,1)} fusion(bf16[512,3072]{1,0:T(8,128)(2,1)S(1)} %copy-done, bf16[3072,1024]{1,0:T(8,128)(2,1)} %param.12), kind=kOutput, calls=%fused_computation.19 | convolution fusion | flops 3221749760 | bytes 10485760 | tf_op jit(solution)/shard_map/dot_general | solution.py:237
  70.5 2.4 copy.37
  72.9 2.4 copy.39
  75.3 1.1 copy.45
  76.4 144.7 %head_attention.1 = bf16[512,3072]{1,0:T(8,128)(2,1)} custom-call(bf16[8,1536,128]{2,1,0:T(8,128)(2,1)} %pad_maximum_fusion.q_hbm, bf16[8,512,128]{2,1,0:T(8,128)(2,1)} %fusion.17.kn_hbm, bf16[8,128,512]{2,1,0:T(8,128)(2,1)} %bitcast.26, bf16[8,512,128]{2,1,0:T(8,128)(2,1)} %bitcast.29, bf16[8,128,512]{2,1,0:T(8,128)(2,1)} %bitcast.28), custom_call_target="tpu_custom_call" | custom-call | tf_op jit(solution)/shard_map/head_attention/pallas_call | solution.py:196
  221.2 0.0 copy-start.1
  221.2 16.0 %convolution_convert_fusion = bf16[512,3072]{1,0:T(8,128)(2,1)} fusion(bf16[512,3072]{1,0:T(8,128)(2,1)} %head_attention.1, bf16[3072,3072]{1,0:T(8,128)(2,1)} %param.13), kind=kOutput, calls=%fused_computation | convolution fusion | flops 9665249280 | bytes 25165824 | tf_op jit(solution)/shard_map/dot_general | solution.py:242
  237.1 0.6 pad_maximum_fusion.1
  237.7 1.6 copy.40
  239.4 2.4 %copy.41 = bf16[512,8,128]{2,1,0:T(8,128)(2,1)} copy(bf16[512,8,128]{0,2,1:T(8,128)(2,1)} %bitcast.27) | data formatting | bytes 2097152
  (9 shorter events, 0.0 us)
Async XLA Ops:
  0.6 2.3 copy-start
  21.6 1.0 copy-start.2
  21.7 1.3 copy-start.4
  70.5 4.8 %copy-start.6 = (bf16[512,8,128]{2,1,0:T(8,128)(2,1)S(1)}, bf16[512,8,128]{2,1,0:T(8,128)(2,1)}, u32[]{:S(2)}) copy-start(bf16[512,8,128]{2,1,0:T(8,128)(2,1)} %param.8) | copy-start | bytes 3145732
  221.1 16.0 %copy-start.3 = (bf16[512,8,64]{2,0,1:T(8,128)(2,1)S(1)}, bf16[512,8,64]{2,0,1:T(8,128)(2,1)}, u32[]{:S(2)}) copy-start(bf16[512,8,64]{2,0,1:T(8,128)(2,1)} %copy-done.2) | copy-start | bytes 1572868
  221.2 16.0 %copy-start.5 = (bf16[512,8,64]{2,0,1:T(8,128)(2,1)S(1)}, bf16[512,8,64]{2,0,1:T(8,128)(2,1)}, u32[]{:S(2)}) copy-start(bf16[512,8,64]{2,0,1:T(8,128)(2,1)} %copy-done.4) | copy-start | bytes 1572868
  221.2 20.6 %copy-start.1 = (bf16[512,3072]{1,0:T(8,128)(2,1)S(1)}, bf16[512,3072]{1,0:T(8,128)(2,1)}, u32[]{:S(2)}) copy-start(bf16[512,3072]{1,0:T(8,128)(2,1)} %param.7) | copy-start | bytes 9437188

commit v2 on v1

v2 whole, which is shorter than its diff:
```python
import functools

import jax
import jax.numpy as jnp
from jax import lax
from jax.experimental import pallas as pl
from jax.experimental.pallas import tpu as pltpu
from jax.sharding import PartitionSpec as P

ROPE_BASE = 500000
MESH_ID = pl.DeviceIdType.MESH
NDEV = 8
NEG = -1e30
LOG2E = 1.4426950408889634
KC, VC, QN, KN, VN = range(5)
NBUF = 3


def rope_tables(positions, head_dim):
    half = jnp.arange(head_dim) % (head_dim // 2)
    inv_freq = 1.0 / (ROPE_BASE ** ((2 * half).astype(jnp.float32) / head_dim))
    angles = positions.astype(jnp.float32)[:, None] * inv_freq[None, :]
    sign = jnp.where(jnp.arange(head_dim) < head_dim // 2, -1.0, 1.0)
    return jnp.cos(angles), jnp.sin(angles) * sign


def layer_kernel(group, tok, scale, x_hbm, wq_hbm, wk_hbm, wv_hbm, cos_hbm, sin_hbm, kc_hbm, vc_hbm, o_hbm, ko_hbm, vo_hbm,
                 x_s, cos_s, sin_s, wbuf, q_send, k_rows, v_rows, q_s, kc_s, vc_raw, vc_t, kn_s, vn_raw, vn_t, acc, m_s, l_s, s_s, osend,
                 in_sem, w_sem, send_sem, recv_sem, osend_sem, orecv_sem):
    y = lax.axis_index('sp')
    xc = lax.axis_index('cp')
    x, c = xc // 2, xc % 2
    me = y * 4 + xc
    c2 = scale * LOG2E
    hd = cos_s.shape[1]
    gw = group * hd
    wide = wbuf.shape[2]

    def peer(k):
        py, px, pc = (y + k // 4) % 2, (x + (k // 2) % 2) % 2, (c + k % 2) % 2
        return py * 4 + px * 2 + pc, (0, py, px * 2 + pc)

    def head_cols(dev):
        return pl.ds(pl.multiple_of(dev * hd, hd), hd)

    def group_cols(dev):
        return pl.ds(pl.multiple_of(dev * gw, gw), gw)

    barrier = pltpu.get_barrier_semaphore()
    for k in range(1, NDEV):
        pl.semaphore_signal(barrier, inc=1, device_id=peer(k)[1], device_id_type=MESH_ID)

    def q_chip(i):
        kc = (i + 1) % 4
        return ((y + kc // 2) % 2) * 2 + (x + kc % 2) % 2

    def w_copy(w_hbm, col, width, t):
        return pltpu.make_async_copy(w_hbm.at[:, pl.ds(pl.multiple_of(col, 256), width)], wbuf.at[t % NBUF, :, pl.ds(0, width)], w_sem.at[t % NBUF])

    def wq_tile(i):
        return w_copy(wq_hbm, q_chip(i) * wide, wide, i)

    def wk_tile(i):
        return w_copy(wk_hbm, i * 512, 512, 4 + i)

    def wv_tile(i):
        return w_copy(wv_hbm, i * 512, 512, 6 + i)

    loads = [pltpu.make_async_copy(x_hbm, x_s, in_sem.at[0]), pltpu.make_async_copy(cos_hbm, cos_s, in_sem.at[1]), pltpu.make_async_copy(sin_hbm, sin_s, in_sem.at[2])]
    loads[0].start()
    wq_tile(0).start()
    loads[1].start()
    loads[2].start()
    wq_tile(1).start()

    def src(kind, dev):
        if kind in (KN, VN):
            return (k_rows if kind == KN else v_rows).at[:, head_cols(dev)]
        return {KC: kc_hbm, VC: vc_hbm, QN: q_send}[kind].at[dev]

    dsts = (kc_s, vc_raw, q_s, kn_s, vn_raw)

    def local(kind):
        slot = me if kind in (KN, VN) else 0
        return pltpu.make_async_copy(src(kind, me), dsts[kind].at[slot], recv_sem.at[kind, 0])

    def remote(kind, k):
        p, did = peer(k)
        slot = me if kind in (KN, VN) else k
        return pltpu.make_async_remote_copy(src_ref=src(kind, p), dst_ref=dsts[kind].at[slot], send_sem=send_sem.at[kind, k],
                                            recv_sem=recv_sem.at[kind, k], device_id=did, device_id_type=MESH_ID)

    def arrived(kind, k):
        slot = peer(k)[0] if kind in (KN, VN) else k
        pltpu.make_async_copy(src(kind, 0), dsts[kind].at[slot], recv_sem.at[kind, k]).wait()

    local(KC).start()
    local(VC).start()
    pl.semaphore_wait(barrier, NDEV - 1)
    order = (1, 2, 4, 6, 3, 5, 7)
    for k in order:
        for kind in (KC, VC):
            remote(kind, k).start()
    acc[...] = jnp.zeros_like(acc)
    l_s[...] = jnp.zeros_like(l_s)
    m_s[...] = jnp.full(m_s.shape, NEG, jnp.float32)
    for cp in loads:
        cp.wait()

    def project(t, n):
        return jnp.dot(x_s[...], wbuf[t % NBUF, :, n * 256:(n + 1) * 256], preferred_element_type=jnp.float32).astype(jnp.bfloat16)

    def rope(rows):
        v = rows.astype(jnp.float32)
        return (v * cos_s[...] + pltpu.roll(v, hd // 2, 1) * sin_s[...]).astype(jnp.bfloat16)

    def q_tile(i, carry):
        @pl.when(i > 0)
        def _():
            for core in range(2):
                kc = i % 4
                remote(QN, 2 * kc + core).start()

        @pl.when(i < 2)
        def _():
            wq_tile(i + 2).start()

        @pl.when(i >= 2)
        def _():
            wk_tile(i - 2).start()

        wq_tile(i).wait()
        chip = q_chip(i)
        for n in range(wide // 256):
            rows = project(i, n)
            for h in range(2):
                head = 2 * n + h
                r = head % group
                q_send[2 * chip + head // group, r * tok:(r + 1) * tok, :] = rope(rows[:, h * hd:(h + 1) * hd])
        return carry

    lax.fori_loop(0, 4, q_tile, 0)

    def k_tile(i, carry):
        wv_tile(i).start()
        wk_tile(i).wait()
        for n in range(2):
            rows = project(4 + i, n)
            for h in range(2):
                k_rows[:, head_cols(4 * i + 2 * n + h)] = rope(rows[:, h * hd:(h + 1) * hd])

        @pl.when(i == 0)
        def _():
            remote(QN, 1).start()
            local(QN).start()
        return carry

    lax.fori_loop(0, 2, k_tile, 0)

    def v_tile(i, carry):
        wv_tile(i).wait()
        for n in range(2):
            v_rows[:, pl.ds(pl.multiple_of(512 * i + 256 * n, 256), 256)] = project(6 + i, n)

        @pl.when(i == 0)
        def _():
            for k in order:
                remote(KN, k).start()
            local(KN).start()
        return carry

    lax.fori_loop(0, 2, v_tile, 0)
    k_out = pltpu.make_async_copy(k_rows, ko_hbm, in_sem.at[0])
    v_out = pltpu.make_async_copy(v_rows, vo_hbm, in_sem.at[1])
    k_out.start()

    def qk(keys, k, r):
        return lax.dot_general(keys, q_s[k, r * tok:(r + 1) * tok, :], (((1,), (1,)), ((), ())), preferred_element_type=jnp.float32)

    def soft_pv(k, r, s, mx, vt):
        cols = slice(r * tok, (r + 1) * tok)
        m_old = m_s[k, :, cols]
        m_new = jnp.maximum(m_old, mx * c2)
        m_s[k, :, cols] = m_new
        alpha = jnp.exp2(m_old - m_new)
        p = jnp.exp2(s * c2 - m_new)
        l_s[k, :, cols] = l_s[k, :, cols] * alpha + jnp.sum(p, axis=0, keepdims=True)
        pv = lax.dot_general(vt, p.astype(jnp.bfloat16), (((1,), (0,)), ((), ())), preferred_element_type=jnp.float32)
        acc[k, :, cols] = acc[k, :, cols] * alpha + pv

    def kchunk(j):
        return kc_s[pl.ds(2 * j, 2)].reshape(2 * tok, hd)

    def cache_chunk(j):
        for core in range(2):
            arrived(KC, 2 * j + core)
            arrived(VC, 2 * j + core)
            vc_t[j, :, core * tok:(core + 1) * tok] = vc_raw[2 * j + core].T

    cache_chunk(0)
    arrived(QN, 0)
    for k in order:
        remote(VN, k).start()
    local(VN).start()
    v_out.start()
    s0 = qk(kchunk(0), 0, 0)
    s_s[0] = s0
    n1 = NDEV * 4

    def phase1(t, mx):
        k, j = t // 4, t % 4
        tn = jnp.minimum(t + 1, n1 - 1)
        kn_, jn_ = tn // 4, tn % 4

        @pl.when(jnp.logical_and(k == 0, j < 3))
        def _():
            cache_chunk(jn_)

        @pl.when(jnp.logical_and(j == 3, k < NDEV - 1))
        def _():
            arrived(QN, kn_)

        for r in range(group):
            nr = (r + 1) % group
            s_next = qk(kchunk(j), k, nr) if nr else qk(kchunk(jn_), kn_, 0)
            cur = s_s[r]
            s_s[nr] = s_next
            soft_pv(k, r, cur, mx, vc_t[j])
            mx = jnp.max(s_next, axis=0, keepdims=True)
        return mx

    lax.fori_loop(0, n1, phase1, jnp.max(s0, axis=0, keepdims=True))

    def new_block(k, carry):
        arrived(KN, k)
        arrived(VN, k)
        dev = peer(k)[0]
        vn_t[dev] = vn_raw[dev].T
        return carry

    lax.fori_loop(0, NDEV, new_block, 0)
    ahead = lax.broadcasted_iota(jnp.int32, (tok, tok), 0) <= lax.broadcasted_iota(jnp.int32, (tok, tok), 1)
    half = pl.ds(0, tok)

    def send_out(k):
        return pltpu.make_async_remote_copy(src_ref=osend.at[k], dst_ref=o_hbm.at[:, group_cols(me)], send_sem=osend_sem.at[k],
                                            recv_sem=orecv_sem.at[k], device_id=peer(k)[1], device_id_type=MESH_ID)

    def phase2(kk, carry):
        k = NDEV - 1 - kk
        p = peer(k)[0]
        s = jnp.where(ahead, qk(kn_s[p], k, 0), NEG)
        s_s[0, half] = s
        mx = jnp.max(s, axis=0, keepdims=True)
        for r in range(group):
            nr = (r + 1) % group
            s_next = jnp.where(ahead, qk(kn_s[p], k, nr), NEG) if nr else qk(kn_s[0], k, 0)
            cur = s_s[r, half]
            s_s[nr, half] = s_next
            soft_pv(k, r, cur, mx, vn_t[p])
            mx = jnp.max(s_next, axis=0, keepdims=True)

        @pl.when(kk > 0)
        def _():
            send_out(k + 1).start()

        def earlier(j, mx):
            jn = jnp.minimum(j + 1, p - 1)
            for r in range(group):
                nr = (r + 1) % group
                s_next = qk(kn_s[j], k, nr) if nr else qk(kn_s[jn], k, 0)
                cur = s_s[r, half]
                s_s[nr, half] = s_next
                soft_pv(k, r, cur, mx, vn_t[j])
                mx = jnp.max(s_next, axis=0, keepdims=True)
            return mx

        lax.fori_loop(0, p, earlier, mx)
        for r in range(group):
            cols = slice(r * tok, (r + 1) * tok)
            o_t = acc[k, :, cols] * (1.0 / l_s[k, :, cols])
            osend[k, :, r * hd:(r + 1) * hd] = o_t.T.astype(jnp.bfloat16)
        return carry

    lax.fori_loop(0, NDEV, phase2, 0)
    own = pltpu.make_async_copy(osend.at[0], o_hbm.at[:, group_cols(me)], orecv_sem.at[0])
    own.start()
    k_out.wait()
    v_out.wait()
    for k in range(1, NDEV):
        for kind in range(5):
            remote(kind, k).wait_send()
        send_out(k).wait_send()
        pltpu.make_async_copy(osend.at[k], o_hbm.at[:, group_cols(peer(k)[0])], orecv_sem.at[k]).wait()
    own.wait()


def layer(x_loc, w_q, w_k, w_v, cos_f, sin_f, kc_t, vc_t):
    kv_heads, tok, hd = kc_t.shape
    d_model = x_loc.shape[1]
    group = w_q.shape[1] // (kv_heads * hd)
    rows = group * tok
    bf, f32 = jnp.bfloat16, jnp.float32
    hbm = pl.BlockSpec(memory_space=pl.ANY)
    sds = jax.ShapeDtypeStruct
    dma = pltpu.SemaphoreType.DMA
    return pl.pallas_call(
        functools.partial(layer_kernel, group, tok, hd ** -0.5),
        out_shape=(sds((tok, kv_heads * group * hd), bf), sds((tok, kv_heads * hd), bf), sds((tok, kv_heads * hd), bf)),
        in_specs=[hbm] * 8,
        out_specs=(hbm, hbm, hbm),
        scratch_shapes=[
            pltpu.VMEM((tok, d_model), bf),
            pltpu.VMEM((tok, hd), f32),
            pltpu.VMEM((tok, hd), f32),
            pltpu.VMEM((NBUF, d_model, 2 * group * hd), bf),
            pltpu.VMEM((NDEV, rows, hd), bf),
            pltpu.VMEM((tok, kv_heads * hd), bf),
            pltpu.VMEM((tok, kv_heads * hd), bf),
            pltpu.VMEM((NDEV, rows, hd), bf),
            pltpu.VMEM((NDEV, tok, hd), bf),
            pltpu.VMEM((NDEV, tok, hd), bf),
            pltpu.VMEM((NDEV // 2, hd, 2 * tok), bf),
            pltpu.VMEM((NDEV, tok, hd), bf),
            pltpu.VMEM((NDEV, tok, hd), bf),
            pltpu.VMEM((NDEV, hd, tok), bf),
            pltpu.VMEM((NDEV, hd, rows), f32),
            pltpu.VMEM((NDEV, 1, rows), f32),
            pltpu.VMEM((NDEV, 1, rows), f32),
            pltpu.VMEM((group, 2 * tok, tok), f32),
            pltpu.VMEM((NDEV, tok, group * hd), bf),
            dma((3,)),
            dma((NBUF,)),
            dma((5, NDEV)),
            dma((5, NDEV)),
            dma((NDEV,)),
            dma((NDEV,)),
        ],
        compiler_params=pltpu.CompilerParams(collective_id=0, has_side_effects=True, vmem_limit_bytes=60 * 2**20),
        name='head_layer',
    )(x_loc, w_q, w_k, w_v, cos_f, sin_f, kc_t, vc_t)


def solution(mesh):
    seq_size = mesh.shape['sp'] * mesh.shape['cp']
    cp_size = mesh.shape['cp']
    row_spec = P(('dp', 'sp', 'cp'))

    def local_fn(x_loc, kc_loc, vc_loc, w_q, w_k, w_v, w_o):
        tok, d_model = x_loc.shape
        cache_loc, kv_heads, hd = kc_loc.shape
        seq_idx = lax.axis_index('sp') * cp_size + lax.axis_index('cp')
        kc_t = jnp.transpose(kc_loc, (1, 0, 2))
        vc_t = jnp.transpose(vc_loc, (1, 0, 2))
        cos_f, sin_f = rope_tables(cache_loc * seq_size + seq_idx * tok + jnp.arange(tok), hd)
        o_rows, k_rows, v_rows = layer(x_loc, w_q, w_k, w_v, cos_f, sin_f, kc_t, vc_t)
        y_loc = jnp.dot(o_rows, w_o, preferred_element_type=jnp.float32).astype(jnp.bfloat16)
        return y_loc, k_rows.reshape(tok, kv_heads, hd), v_rows.reshape(tok, kv_heads, hd)

    return jax.shard_map(local_fn, mesh=mesh, in_specs=(row_spec, row_spec, row_spec, P(), P(), P(), P()), out_specs=(row_spec, row_spec, row_spec), check_vma=False)
```

time: 242 us -> 162 us (0.67)
  local copies, waits for them, and re-layouts: 35.2 us -> 5.73 us
  matrix products: 45.2 us -> 16.1 us
  other arithmetic: 16 us -> 1.84 us
  Pallas kernels: 145 us -> 137 us
    dot_general x3 -> x0, matrix products: 29.2 us -> none  [the longest x1 14.9 us: local_fn(): jnp.dot(x_loc, w_q, preferred_element_type=jnp.float32).astype(jnp.bfloat16)]
    unnamed x20 -> x6, local copies, waits for them, and re-layouts: 13.7 us -> 2.5 us
    convert_element_type x3 -> x0, local copies, waits for them, and re-layouts: 9.29 us -> none  [the longest x1 4.65 us: local_fn(): jnp.dot(x_loc, w_q, preferred_element_type=jnp.float32).astype(jnp.bfloat16)]
    another operation x2 -> x0, local copies, waits for them, and re-layouts: 8.32 us -> none
    pallas_call x1, Pallas kernels: 145 us -> 137 us  [layer(): pl.pallas_call(functools.partial(layer_kernel, group, tok, hd ** (-0.5)),...]
    another operation x2 -> x0, other arithmetic: 7.08 us -> none
    concatenate x2 -> x0, other arithmetic: 6.83 us -> none  [apply_rope(): jnp.concatenate([lo_half * cos_t - hi_half * sin_t, hi_half * cos_t + lo_...]
    transpose x0 -> x1, local copies, waits for them, and re-layouts: none -> 3.23 us  [local_fn(): vc_t = jnp.transpose(vc_loc, (1, 0, 2))]
where the time goes in v2:
time: 162 us
  Pallas kernels  137 us (85%)
  matrix products  16.1 us (10%)
  local copies, waits for them, and re-layouts  5.73 us (4%)
  other arithmetic  1.84 us (1%)
    pallas_call x1, Pallas kernels, layer(): pl.pallas_call(functools.partial(layer_kernel, group, tok, hd ** (-0.5)),...  137 us
    dot_general x1, matrix products, local_fn(): jnp.dot(o_rows, w_o, preferred_element_type=jnp.float32)  16.1 us

profile of v2, /device:TPU:0, one launch (start us, length us, event | category | flops | bytes accessed | tf_op | source)
XLA Modules:
  0.0 161.6 jit_solution(7464662318887638142)
XLA Ops:
  0.7 1.8 %fusion = (f32[512,128]{1,0:T(8,128)}, f32[512,128]{1,0:T(8,128)}) fusion(f32[128]{0:T(128)S(1)} %get-tuple-element.11, f32[128]{0:T(128)S(1)} %get-tuple-element.12, f32[512]{0:T(512)S(1)} %add_convert_fusion), kind=kLoop, calls=%fused_computation.5 | loop fusion | flops 131072 | bytes 527360 | tf_op jit(solution)/shard_map/mul | solution.py:24
  2.5 3.2 %copy_bitcast_fusion = (bf16[8,512,128]{2,1,0:T(8,128)(2,1)}, bf16[8,512,128]{2,1,0:T(8,128)(2,1)}) fusion(bf16[512,8,128]{2,1,0:T(8,128)(2,1)} %param.9, bf16[512,8,128]{2,1,0:T(8,128)(2,1)} %param.8), kind=kLoop, calls=%fused_computation.1 | loop fusion | bytes 4194304 | tf_op jit(solution)/shard_map/transpose | solution.py:354
  5.7 137.2 %head_layer.1 = (bf16[512,3072]{1,0:T(8,128)(2,1)}, bf16[512,1024]{1,0:T(8,128)(2,1)}, bf16[512,1024]{1,0:T(8,128)(2,1)}) custom-call(bf16[512,3072]{1,0:T(8,128)(2,1)} %x_hbm.1, bf16[3072,3072]{1,0:T(8,128)(2,1)} %wq_hbm.1, bf16[3072,1024]{1,0:T(8,128)(2,1)} %wk_hbm.1, bf16[3072,1024]{1,0:T(8,128)(2,1)} %wv_hbm.1, f32[512,128]{1,0:T(8,128)} %get-tuple-element.10.cos_hbm, ...), custom_call_target="tpu_custom_call" | custom-call | tf_op jit(solution)/shard_map/head_layer/pallas_call | solution.py:307
  142.9 0.0 copy-start.1
  143.0 0.0 copy-start
  143.0 16.1 %convolution_convert_fusion = bf16[512,3072]{1,0:T(8,128)(2,1)} fusion(bf16[512,3072]{1,0:T(8,128)(2,1)} %get-tuple-element.6, bf16[3072,3072]{1,0:T(8,128)(2,1)} %param.13), kind=kOutput, calls=%fused_computation | convolution fusion | flops 9665249280 | bytes 25165824 | tf_op jit(solution)/shard_map/dot_general | solution.py:357
  159.1 0.0 copy-done.1
  159.1 1.2 copy.12
  160.3 0.0 copy-done
  160.3 1.2 copy.13
  (2 shorter events, 0.0 us)
Async XLA Ops:
  142.9 16.1 %copy-start.1 = (bf16[512,1024]{1,0:T(8,128)(2,1)S(1)}, bf16[512,1024]{1,0:T(8,128)(2,1)}, u32[]{:S(2)}) copy-start(bf16[512,1024]{1,0:T(8,128)(2,1)} %get-tuple-element.7) | copy-start | bytes 3145732
  143.0 17.4 %copy-start = (bf16[512,1024]{1,0:T(8,128)(2,1)S(1)}, bf16[512,1024]{1,0:T(8,128)(2,1)}, u32[]{:S(2)}) copy-start(bf16[512,1024]{1,0:T(8,128)(2,1)} %get-tuple-element.8) | copy-start | bytes 3145732

commit v3 on v2

--- a/solution.py
+++ b/solution.py
@@ -13,7 +13,7 @@
 NEG = -1e30
 LOG2E = 1.4426950408889634
 KC, VC, QN, KN, VN = range(5)
-NBUF = 3
+NBUF = 4
 
 
 def rope_tables(positions, head_dim):
@@ -24,8 +24,8 @@
     return jnp.cos(angles), jnp.sin(angles) * sign
 
 
-def layer_kernel(group, tok, scale, x_hbm, wq_hbm, wk_hbm, wv_hbm, cos_hbm, sin_hbm, kc_hbm, vc_hbm, o_hbm, ko_hbm, vo_hbm,
-                 x_s, cos_s, sin_s, wbuf, q_send, k_rows, v_rows, q_s, kc_s, vc_raw, vc_t, kn_s, vn_raw, vn_t, acc, m_s, l_s, s_s, osend,
+def layer_kernel(group, tok, scale, x_hbm, wq_hbm, wk_hbm, wv_hbm, wo_hbm, cos_hbm, sin_hbm, kc_hbm, vc_hbm, y_hbm, ko_hbm, vo_hbm,
+                 x_s, cos_s, sin_s, wbuf, q_send, k_rows, v_rows, q_s, kc_s, vc_raw, vc_t, kn_s, vn_raw, vn_t, acc, m_s, l_s, s_s, osend, o_s,
                  in_sem, w_sem, send_sem, recv_sem, osend_sem, orecv_sem):
     y = lax.axis_index('sp')
     xc = lax.axis_index('cp')
@@ -65,6 +65,9 @@
 
     def wv_tile(i):
         return w_copy(wv_hbm, i * 512, 512, 6 + i)
+
+    def wo_tile(n):
+        return w_copy(wo_hbm, n * wide, wide, n)
 
     loads = [pltpu.make_async_copy(x_hbm, x_s, in_sem.at[0]), pltpu.make_async_copy(cos_hbm, cos_s, in_sem.at[1]), pltpu.make_async_copy(sin_hbm, sin_s, in_sem.at[2])]
     loads[0].start()
@@ -112,14 +115,13 @@
 
     def rope(rows):
         v = rows.astype(jnp.float32)
-        return (v * cos_s[...] + pltpu.roll(v, hd // 2, 1) * sin_s[...]).astype(jnp.bfloat16)
+        return v * cos_s[...] + pltpu.roll(v, hd // 2, 1) * sin_s[...]
 
     def q_tile(i, carry):
-        @pl.when(i > 0)
+        @pl.when(jnp.logical_and(i > 0, i < 3))
         def _():
             for core in range(2):
-                kc = i % 4
-                remote(QN, 2 * kc + core).start()
+                remote(QN, 2 * i + core).start()
 
         @pl.when(i < 2)
         def _():
@@ -136,7 +138,7 @@
             for h in range(2):
                 head = 2 * n + h
                 r = head % group
-                q_send[2 * chip + head // group, r * tok:(r + 1) * tok, :] = rope(rows[:, h * hd:(h + 1) * hd])
+                q_send[2 * chip + head // group, r * tok:(r + 1) * tok, :] = (rope(rows[:, h * hd:(h + 1) * hd]) * c2).astype(jnp.bfloat16)
         return carry
 
     lax.fori_loop(0, 4, q_tile, 0)
@@ -147,7 +149,7 @@
         for n in range(2):
             rows = project(4 + i, n)
             for h in range(2):
-                k_rows[:, head_cols(4 * i + 2 * n + h)] = rope(rows[:, h * hd:(h + 1) * hd])
+                k_rows[:, head_cols(4 * i + 2 * n + h)] = rope(rows[:, h * hd:(h + 1) * hd]).astype(jnp.bfloat16)
 
         @pl.when(i == 0)
         def _():
@@ -180,10 +182,10 @@
     def soft_pv(k, r, s, mx, vt):
         cols = slice(r * tok, (r + 1) * tok)
         m_old = m_s[k, :, cols]
-        m_new = jnp.maximum(m_old, mx * c2)
+        m_new = jnp.maximum(m_old, mx)
         m_s[k, :, cols] = m_new
         alpha = jnp.exp2(m_old - m_new)
-        p = jnp.exp2(s * c2 - m_new)
+        p = jnp.exp2(s - m_new)
         l_s[k, :, cols] = l_s[k, :, cols] * alpha + jnp.sum(p, axis=0, keepdims=True)
         pv = lax.dot_general(vt, p.astype(jnp.bfloat16), (((1,), (0,)), ((), ())), preferred_element_type=jnp.float32)
         acc[k, :, cols] = acc[k, :, cols] * alpha + pv
@@ -197,39 +199,46 @@
             arrived(VC, 2 * j + core)
             vc_t[j, :, core * tok:(core + 1) * tok] = vc_raw[2 * j + core].T
 
+    for n in range(4):
+        wo_tile(n).start()
     cache_chunk(0)
     arrived(QN, 0)
     for k in order:
         remote(VN, k).start()
+    for k in (6, 7):
+        remote(QN, k).start()
     local(VN).start()
     v_out.start()
-    s0 = qk(kchunk(0), 0, 0)
-    s_s[0] = s0
-    n1 = NDEV * 4
-
-    def phase1(t, mx):
-        k, j = t // 4, t % 4
-        tn = jnp.minimum(t + 1, n1 - 1)
-        kn_, jn_ = tn // 4, tn % 4
-
-        @pl.when(jnp.logical_and(k == 0, j < 3))
-        def _():
-            cache_chunk(jn_)
-
-        @pl.when(jnp.logical_and(j == 3, k < NDEV - 1))
-        def _():
-            arrived(QN, kn_)
-
-        for r in range(group):
-            nr = (r + 1) % group
-            s_next = qk(kchunk(j), k, nr) if nr else qk(kchunk(jn_), kn_, 0)
-            cur = s_s[r]
-            s_s[nr] = s_next
-            soft_pv(k, r, cur, mx, vc_t[j])
-            mx = jnp.max(s_next, axis=0, keepdims=True)
-        return mx
-
-    lax.fori_loop(0, n1, phase1, jnp.max(s0, axis=0, keepdims=True))
+    def cache_part(first, count, waits):
+        s0 = qk(kchunk(0), first, 0)
+        s_s[0] = s0
+        steps = 4 * count
+
+        def step(t, mx):
+            k, j = first + t // 4, t % 4
+            tn = jnp.minimum(t + 1, steps - 1)
+            k_next, j_next = first + tn // 4, tn % 4
+            if waits:
+                @pl.when(t < 3)
+                def _():
+                    cache_chunk(j_next)
+
+                @pl.when(jnp.logical_and(j == 3, t < steps - 1))
+                def _():
+                    arrived(QN, k_next)
+
+            for r in range(group):
+                nr = (r + 1) % group
+                s_next = qk(kchunk(j), k, nr) if nr else qk(kchunk(j_next), k_next, 0)
+                cur = s_s[r]
+                s_s[nr] = s_next
+                soft_pv(k, r, cur, mx, vc_t[j])
+                mx = jnp.max(s_next, axis=0, keepdims=True)
+            return mx
+
+        lax.fori_loop(0, steps, step, jnp.max(s0, axis=0, keepdims=True))
+
+    cache_part(0, 6, True)
 
     def new_block(k, carry):
         arrived(KN, k)
@@ -243,12 +252,24 @@
     half = pl.ds(0, tok)
 
     def send_out(k):
-        return pltpu.make_async_remote_copy(src_ref=osend.at[k], dst_ref=o_hbm.at[:, group_cols(me)], send_sem=osend_sem.at[k],
+        return pltpu.make_async_remote_copy(src_ref=osend.at[k], dst_ref=o_s.at[k // 2, :, group_cols(c)], send_sem=osend_sem.at[k],
                                             recv_sem=orecv_sem.at[k], device_id=peer(k)[1], device_id_type=MESH_ID)
 
-    def phase2(kk, carry):
-        k = NDEV - 1 - kk
+    def out_arrived(k):
+        pltpu.make_async_copy(osend.at[k], o_s.at[k // 2, :, group_cols(peer(k)[0] % 2)], orecv_sem.at[k]).wait()
+
+    def item(i):
+        return i + 2 - (i // 6) * (2 * i - 5)
+
+    def phase2(i, carry):
+        k = item(i)
         p = peer(k)[0]
+
+        @pl.when(i // 2 == 2)
+        def _():
+            arrived(QN, k)
+            cache_part(k, 1, False)
+
         s = jnp.where(ahead, qk(kn_s[p], k, 0), NEG)
         s_s[0, half] = s
         mx = jnp.max(s, axis=0, keepdims=True)
@@ -260,9 +281,9 @@
             soft_pv(k, r, cur, mx, vn_t[p])
             mx = jnp.max(s_next, axis=0, keepdims=True)
 
-        @pl.when(kk > 0)
-        def _():
-            send_out(k + 1).start()
+        @pl.when(i > 0)
+        def _():
+            send_out(item(i - 1)).start()
 
         def earlier(j, mx):
             jn = jnp.minimum(j + 1, p - 1)
@@ -283,19 +304,64 @@
         return carry
 
     lax.fori_loop(0, NDEV, phase2, 0)
-    own = pltpu.make_async_copy(osend.at[0], o_hbm.at[:, group_cols(me)], orecv_sem.at[0])
-    own.start()
+
+    own = pltpu.make_async_copy(osend.at[0], o_s.at[0, :, group_cols(c)], orecv_sem.at[0])
+    for n in range(4):
+        wo_tile(n).wait()
     k_out.wait()
     v_out.wait()
+    quarter = tok // 4
+
+    def y_piece(kc, old, last):
+        chip = ((y + kc // 2) % 2) * 2 + (x + kc % 2) % 2
+        w_rows = pl.ds(pl.multiple_of(chip * wide, wide), wide)
+
+        def tiles(n, carry):
+            for sub in range(3):
+                val = jnp.dot(o_s[kc], wbuf[n, w_rows, sub * 256:(sub + 1) * 256], preferred_element_type=jnp.float32)
+                if old:
+                    val = val + jnp.concatenate([acc[2 * n + (4 * sub + u) // 6, :, (4 * sub + u) % 6 * 256:(4 * sub + u) % 6 * 256 + 256] for u in range(4)], axis=0)
+                if last:
+                    x_s[:, pl.ds(pl.multiple_of(n * wide + sub * 256, 256), 256)] = val.astype(jnp.bfloat16)
+                else:
+                    for u in range(4):
+                        f = 4 * sub + u
+                        acc[2 * n + f // 6, :, f % 6 * 256:f % 6 * 256 + 256] = val[u * quarter:(u + 1) * quarter]
+            if last:
+                @pl.when(n > 0)
+                def _():
+                    y_copy(n - 1).start()
+            return carry
+
+        lax.fori_loop(0, 4, tiles, 0)
+
+    def y_copy(n):
+        cols = pl.ds(pl.multiple_of(n * wide, wide), wide)
+        return pltpu.make_async_copy(x_s.at[:, cols], y_hbm.at[:, cols], w_sem.at[n])
+
+    out_arrived(2)
+    out_arrived(3)
+    y_piece(1, False, False)
+    own.start()
+    out_arrived(4)
+    out_arrived(5)
+    y_piece(2, True, False)
+    out_arrived(1)
+    own.wait()
+    y_piece(0, True, False)
+    out_arrived(6)
+    out_arrived(7)
+    y_piece(3, True, True)
     for k in range(1, NDEV):
         for kind in range(5):
             remote(kind, k).wait_send()
         send_out(k).wait_send()
-        pltpu.make_async_copy(osend.at[k], o_hbm.at[:, group_cols(peer(k)[0])], orecv_sem.at[k]).wait()
-    own.wait()
-
-
-def layer(x_loc, w_q, w_k, w_v, cos_f, sin_f, kc_t, vc_t):
+    y_copy(3).start()
+    for n in range(4):
+        y_copy(n).wait()
+
+
+def layer(x_loc, w_q, w_k, w_v, w_o, cos_f, sin_f, kc_t, vc_t):
     kv_heads, tok, hd = kc_t.shape
     d_model = x_loc.shape[1]
     group = w_q.shape[1] // (kv_heads * hd)
@@ -306,8 +372,8 @@
     dma = pltpu.SemaphoreType.DMA
     return pl.pallas_call(
         functools.partial(layer_kernel, group, tok, hd ** -0.5),
-        out_shape=(sds((tok, kv_heads * group * hd), bf), sds((tok, kv_heads * hd), bf), sds((tok, kv_heads * hd), bf)),
-        in_specs=[hbm] * 8,
+        out_shape=(sds((tok, d_model), bf), sds((tok, kv_heads * hd), bf), sds((tok, kv_heads * hd), bf)),
+        in_specs=[hbm] * 9,
         out_specs=(hbm, hbm, hbm),
         scratch_shapes=[
             pltpu.VMEM((tok, d_model), bf),
@@ -329,6 +395,7 @@
             pltpu.VMEM((NDEV, 1, rows), f32),
             pltpu.VMEM((group, 2 * tok, tok), f32),
             pltpu.VMEM((NDEV, tok, group * hd), bf),
+            pltpu.VMEM((NDEV // 2, tok, 2 * group * hd), bf),
             dma((3,)),
             dma((NBUF,)),
             dma((5, NDEV)),
@@ -336,9 +403,9 @@
             dma((NDEV,)),
             dma((NDEV,)),
         ],
-        compiler_params=pltpu.CompilerParams(collective_id=0, has_side_effects=True, vmem_limit_bytes=60 * 2**20),
+        compiler_params=pltpu.CompilerParams(collective_id=0, has_side_effects=True, vmem_limit_bytes=63 * 2**20),
         name='head_layer',
-    )(x_loc, w_q, w_k, w_v, cos_f, sin_f, kc_t, vc_t)
+    )(x_loc, w_q, w_k, w_v, w_o, cos_f, sin_f, kc_t, vc_t)
 
 
 def solution(mesh):
@@ -353,8 +420,7 @@
         kc_t = jnp.transpose(kc_loc, (1, 0, 2))
         vc_t = jnp.transpose(vc_loc, (1, 0, 2))
         cos_f, sin_f = rope_tables(cache_loc * seq_size + seq_idx * tok + jnp.arange(tok), hd)
-        o_rows, k_rows, v_rows = layer(x_loc, w_q, w_k, w_v, cos_f, sin_f, kc_t, vc_t)
-        y_loc = jnp.dot(o_rows, w_o, preferred_element_type=jnp.float32).astype(jnp.bfloat16)
+        y_loc, k_rows, v_rows = layer(x_loc, w_q, w_k, w_v, w_o, cos_f, sin_f, kc_t, vc_t)
         return y_loc, k_rows.reshape(tok, kv_heads, hd), v_rows.reshape(tok, kv_heads, hd)
 
     return jax.shard_map(local_fn, mesh=mesh, in_specs=(row_spec, row_spec, row_spec, P(), P(), P(), P()), out_specs=(row_spec, row_spec, row_spec), check_vma=False)

time: 162 us -> 145 us (0.90)
  matrix products: 16.1 us -> 0 us
  Pallas kernels: 137 us -> 132 us
  local copies, waits for them, and re-layouts: 5.73 us -> 9.99 us
    dot_general x1 -> x0, matrix products: 16.1 us -> none  [local_fn(): jnp.dot(o_rows, w_o, preferred_element_type=jnp.float32)]
    pallas_call x1, Pallas kernels: 137 us -> 132 us  [layer(): pl.pallas_call(functools.partial(layer_kernel, group, tok, hd ** (-0.5)),...]
    unnamed x6 -> x5, local copies, waits for them, and re-layouts: 2.5 us -> 6.76 us
where the time goes in v3:
time: 145 us; the launch traced here: 144 us
  Pallas kernels  132 us (91%)
  local copies, waits for them, and re-layouts  9.99 us (7%)
  other arithmetic  1.84 us (1%)
    pallas_call x1, Pallas kernels, layer(): pl.pallas_call(functools.partial(layer_kernel, group, tok, hd ** (-0.5)),...  132 us
    unnamed x5, local copies, waits for them, and re-layouts  6.76 us
    transpose x1, local copies, waits for them, and re-layouts, local_fn(): vc_t = jnp.transpose(vc_loc, (1, 0, 2))  3.23 us

profile of v3, /device:TPU:0, one launch (start us, length us, event | category | flops | bytes accessed | tf_op | source)
XLA Modules:
  0.0 144.3 jit_solution(4005216622553952873)
XLA Ops:
  0.7 1.8 %fusion = (f32[512,128]{1,0:T(8,128)}, f32[512,128]{1,0:T(8,128)}) fusion(f32[128]{0:T(128)S(1)} %get-tuple-element.11, f32[128]{0:T(128)S(1)} %get-tuple-element.12, f32[512]{0:T(512)S(1)} %add_convert_fusion), kind=kLoop, calls=%fused_computation.4 | loop fusion | flops 131072 | bytes 527360 | tf_op jit(solution)/shard_map/mul | solution.py:24
  2.5 3.2 %copy_bitcast_fusion = (bf16[8,512,128]{2,1,0:T(8,128)(2,1)}, bf16[8,512,128]{2,1,0:T(8,128)(2,1)}) fusion(bf16[512,8,128]{2,1,0:T(8,128)(2,1)} %param.9, bf16[512,8,128]{2,1,0:T(8,128)(2,1)} %param.8), kind=kLoop, calls=%fused_computation | loop fusion | bytes 4194304 | tf_op jit(solution)/shard_map/transpose | solution.py:421
  5.7 131.8 %head_layer.1 = (bf16[512,3072]{1,0:T(8,128)(2,1)}, bf16[512,1024]{1,0:T(8,128)(2,1)}, bf16[512,1024]{1,0:T(8,128)(2,1)}) custom-call(bf16[512,3072]{1,0:T(8,128)(2,1)} %x_hbm.1, bf16[3072,3072]{1,0:T(8,128)(2,1)} %wq_hbm.1, bf16[3072,1024]{1,0:T(8,128)(2,1)} %wk_hbm.1, bf16[3072,1024]{1,0:T(8,128)(2,1)} %wv_hbm.1, bf16[3072,3072]{1,0:T(8,128)(2,1)} %wo_hbm.1, ...), custom_call_target="tpu_custom_call" | custom-call | tf_op jit(solution)/shard_map/head_layer/pallas_call | solution.py:373
  137.6 0.0 copy-start
  137.6 2.6 %copy.12 = bf16[64,8,8,128]{3,2,1,0:T(8,128)(2,1)} copy(bf16[64,8,8,128]{3,1,2,0:T(8,128)(2,1)} %bitcast.11) | data formatting | bytes 2097152
  140.2 2.5 %copy.13 = bf16[64,8,8,128]{3,2,1,0:T(8,128)(2,1)} copy(bf16[64,8,8,128]{3,1,2,0:T(8,128)(2,1)} %bitcast.10) | data formatting | bytes 2097152
  142.7 0.0 copy-done
  142.7 1.7 %copy.17 = bf16[512,3072]{1,0:T(8,128)(2,1)} copy(bf16[512,3072]{1,0:T(8,128)(2,1)S(1)} %copy-done) | data formatting | bytes 6291456
  (2 shorter events, 0.0 us)
Async XLA Ops:
  137.6 5.1 %copy-start = (bf16[512,3072]{1,0:T(8,128)(2,1)S(1)}, bf16[512,3072]{1,0:T(8,128)(2,1)}, u32[]{:S(2)}) copy-start(bf16[512,3072]{1,0:T(8,128)(2,1)} %get-tuple-element.18) | copy-start | bytes 9437188

commit v4 on v3

--- a/solution.py
+++ b/solution.py
@@ -2,6 +2,7 @@
 
 import jax
 import jax.numpy as jnp
+import numpy as np
 from jax import lax
 from jax.experimental import pallas as pl
 from jax.experimental.pallas import tpu as pltpu
@@ -16,16 +17,15 @@
 NBUF = 4
 
 
-def rope_tables(positions, head_dim):
-    half = jnp.arange(head_dim) % (head_dim // 2)
-    inv_freq = 1.0 / (ROPE_BASE ** ((2 * half).astype(jnp.float32) / head_dim))
-    angles = positions.astype(jnp.float32)[:, None] * inv_freq[None, :]
-    sign = jnp.where(jnp.arange(head_dim) < head_dim // 2, -1.0, 1.0)
-    return jnp.cos(angles), jnp.sin(angles) * sign
-
-
-def layer_kernel(group, tok, scale, x_hbm, wq_hbm, wk_hbm, wv_hbm, wo_hbm, cos_hbm, sin_hbm, kc_hbm, vc_hbm, y_hbm, ko_hbm, vo_hbm,
-                 x_s, cos_s, sin_s, wbuf, q_send, k_rows, v_rows, q_s, kc_s, vc_raw, vc_t, kn_s, vn_raw, vn_t, acc, m_s, l_s, s_s, osend, o_s,
+def rope_table(first, count, head_dim):
+    f32 = np.float32
+    inv_freq = f32(1.0) / (f32(ROPE_BASE) ** (np.arange(0, head_dim, 2, dtype=f32) / f32(head_dim)))
+    angles = (first + np.arange(count)).astype(f32)[:, None] * inv_freq[None, :]
+    return np.concatenate([np.cos(angles.astype(np.float64)), np.sin(angles.astype(np.float64))], axis=1).astype(f32)
+
+
+def layer_kernel(group, tok, scale, x_hbm, wq_hbm, wk_hbm, wv_hbm, wo_hbm, table_hbm, kc_hbm, vc_hbm, y_hbm, ko_hbm, vo_hbm,
+                 x_s, cos_s, sin_s, wbuf, q_send, k_rows, v_rows, q_s, kc_s, vc_raw, vc_t, kn_s, vn_raw, vn_t, acc, m_s, l_s, s_s, osend, o_s, kc_out, vc_out,
                  in_sem, w_sem, send_sem, recv_sem, osend_sem, orecv_sem):
     y = lax.axis_index('sp')
     xc = lax.axis_index('cp')
@@ -69,17 +69,17 @@
     def wo_tile(n):
         return w_copy(wo_hbm, n * wide, wide, n)
 
-    loads = [pltpu.make_async_copy(x_hbm, x_s, in_sem.at[0]), pltpu.make_async_copy(cos_hbm, cos_s, in_sem.at[1]), pltpu.make_async_copy(sin_hbm, sin_s, in_sem.at[2])]
-    loads[0].start()
+    loads = [pltpu.make_async_copy(x_hbm, x_s, in_sem.at[0]), pltpu.make_async_copy(table_hbm.at[pl.ds(pl.multiple_of(me * tok, tok), tok)], cos_s, in_sem.at[1])]
+    raw = [pltpu.make_async_copy(hbm, osend.at[:, :, pl.ds(n * hd, hd)], in_sem.at[2 + n]) for n, hbm in enumerate((kc_hbm, vc_hbm))]
+    for cp in raw + loads:
+        cp.start()
     wq_tile(0).start()
-    loads[1].start()
-    loads[2].start()
     wq_tile(1).start()
 
     def src(kind, dev):
         if kind in (KN, VN):
             return (k_rows if kind == KN else v_rows).at[:, head_cols(dev)]
-        return {KC: kc_hbm, VC: vc_hbm, QN: q_send}[kind].at[dev]
+        return {KC: kc_out, VC: vc_out, QN: q_send}[kind].at[dev]
 
     dsts = (kc_s, vc_raw, q_s, kn_s, vn_raw)
 
@@ -97,9 +97,16 @@
         slot = peer(k)[0] if kind in (KN, VN) else k
         pltpu.make_async_copy(src(kind, 0), dsts[kind].at[slot], recv_sem.at[kind, k]).wait()
 
+    for n, out in enumerate((kc_out, vc_out)):
+        raw[n].wait()
+        for b in range(NDEV):
+            s_s[n, b // 4, b % 4 * tok:(b % 4 + 1) * tok, :] = osend[b, :, n * hd:(n + 1) * hd].astype(jnp.float32)
+        for h in range(NDEV):
+            for g in range(2):
+                out[h, g * tok // 2:(g + 1) * tok // 2, :] = s_s[n, g, pl.ds(h, tok // 2, stride=NDEV), :].astype(jnp.bfloat16)
+    pl.semaphore_wait(barrier, NDEV - 1)
     local(KC).start()
     local(VC).start()
-    pl.semaphore_wait(barrier, NDEV - 1)
     order = (1, 2, 4, 6, 3, 5, 7)
     for k in order:
         for kind in (KC, VC):
@@ -109,6 +116,11 @@
     m_s[...] = jnp.full(m_s.shape, NEG, jnp.float32)
     for cp in loads:
         cp.wait()
+    table = cos_s[...]
+    turned = pltpu.roll(table, hd // 2, 1)
+    low = lax.broadcasted_iota(jnp.int32, table.shape, 1) < hd // 2
+    cos_s[...] = jnp.where(low, table, turned)
+    sin_s[...] = jnp.where(low, -turned, table)
 
     def project(t, n):
         return jnp.dot(x_s[...], wbuf[t % NBUF, :, n * 256:(n + 1) * 256], preferred_element_type=jnp.float32).astype(jnp.bfloat16)
@@ -172,26 +184,73 @@
         return carry
 
     lax.fori_loop(0, 2, v_tile, 0)
-    k_out = pltpu.make_async_copy(k_rows, ko_hbm, in_sem.at[0])
-    v_out = pltpu.make_async_copy(v_rows, vo_hbm, in_sem.at[1])
-    k_out.start()
-
-    def qk(keys, k, r):
-        return lax.dot_general(keys, q_s[k, r * tok:(r + 1) * tok, :], (((1,), (1,)), ((), ())), preferred_element_type=jnp.float32)
-
-    def soft_pv(k, r, s, mx, vt):
-        cols = slice(r * tok, (r + 1) * tok)
+    news = [pltpu.make_async_copy(osend.at[:, :, pl.ds(n * hd, hd)], hbm, in_sem.at[2 + n]) for n, hbm in enumerate((ko_hbm, vo_hbm))]
+    for n, rows in enumerate((k_rows, v_rows)):
+        for h in range(NDEV):
+            for g in range(2):
+                s_s[n, g, pl.ds(h, tok // 2, stride=NDEV), :] = rows[g * tok // 2:(g + 1) * tok // 2, h * hd:(h + 1) * hd].astype(jnp.float32)
+        for b in range(NDEV):
+            osend[b, :, n * hd:(n + 1) * hd] = s_s[n, b // 4, b % 4 * tok:(b % 4 + 1) * tok, :].astype(jnp.bfloat16)
+
+    for n in range(4):
+        wo_tile(n).start()
+    for k in order:
+        remote(VN, k).start()
+    for k in (6, 7):
+        remote(QN, k).start()
+    local(VN).start()
+    for cp in news:
+        cp.start()
+    def qk(keys, k, rows):
+        return lax.dot_general(keys, q_s[k, rows, :], (((1,), (1,)), ((), ())), preferred_element_type=jnp.float32)
+
+    def slab(u, j, rows, cols):
+        return j % 2, pl.ds((u * (cols // 256) + j // 2) * rows, rows)
+
+    def put(slot, u, val):
+        rows, cols = val.shape
+        for j in range(cols // 128):
+            side, where = slab(u, j, rows, cols)
+            s_s[slot, side, where, :] = val[:, j * 128:(j + 1) * 128]
+
+    def get(slot, u, rows, cols):
+        parts = []
+        for j in range(cols // 128):
+            side, where = slab(u, j, rows, cols)
+            parts.append(s_s[slot, side, where, :])
+        return jnp.concatenate(parts, axis=1)
+
+    def tile_max(old, val):
+        top = jnp.max(val, axis=0, keepdims=True)
+        return top if old is None else jnp.maximum(old, top)
+
+    def sub_step(slot, k, cols, size, mx, pieces, depth, vt, following):
         m_old = m_s[k, :, cols]
         m_new = jnp.maximum(m_old, mx)
         m_s[k, :, cols] = m_new
         alpha = jnp.exp2(m_old - m_new)
-        p = jnp.exp2(s - m_new)
-        l_s[k, :, cols] = l_s[k, :, cols] * alpha + jnp.sum(p, axis=0, keepdims=True)
-        pv = lax.dot_general(vt, p.astype(jnp.bfloat16), (((1,), (0,)), ((), ())), preferred_element_type=jnp.float32)
+        total, pv, mx_next = None, None, None
+        for u in range(pieces):
+            s_next = None if following is None else following(u)
+            p = jnp.exp2(get(slot, u, depth, size) - m_new)
+            if s_next is not None:
+                put(1 - slot, u, s_next)
+                mx_next = tile_max(mx_next, s_next)
+            part = jnp.sum(p, axis=0, keepdims=True)
+            prod = jnp.dot(vt(u), p.astype(jnp.bfloat16), preferred_element_type=jnp.float32)
+            total = part if total is None else total + part
+            pv = prod if pv is None else pv + prod
+        l_s[k, :, cols] = l_s[k, :, cols] * alpha + total
         acc[k, :, cols] = acc[k, :, cols] * alpha + pv
-
-    def kchunk(j):
-        return kc_s[pl.ds(2 * j, 2)].reshape(2 * tok, hd)
+        return mx_next
+
+    def first_tile(pieces, scores):
+        mx = None
+        for u in range(pieces):
+            val = scores(u)
+            put(0, u, val)
+            mx = tile_max(mx, val)
+        return mx
 
     def cache_chunk(j):
         for core in range(2):
@@ -199,46 +258,45 @@
             arrived(VC, 2 * j + core)
             vc_t[j, :, core * tok:(core + 1) * tok] = vc_raw[2 * j + core].T
 
-    for n in range(4):
-        wo_tile(n).start()
-    cache_chunk(0)
-    arrived(QN, 0)
-    for k in order:
-        remote(VN, k).start()
-    for k in (6, 7):
-        remote(QN, k).start()
-    local(VN).start()
-    v_out.start()
-    def cache_part(first, count, waits):
-        s0 = qk(kchunk(0), first, 0)
-        s_s[0] = s0
-        steps = 4 * count
+    def cache_part(first, count):
+        pieces = NDEV // 2
+        steps = 2 * count
+        mx0 = first_tile(pieces, lambda u: qk(kc_s[u], first, pl.ds(0, 256)))
 
         def step(t, mx):
-            k, j = first + t // 4, t % 4
+            k, half = first + t // 2, t % 2
             tn = jnp.minimum(t + 1, steps - 1)
-            k_next, j_next = first + tn // 4, tn % 4
-            if waits:
-                @pl.when(t < 3)
-                def _():
-                    cache_chunk(j_next)
-
-                @pl.when(jnp.logical_and(j == 3, t < steps - 1))
-                def _():
-                    arrived(QN, k_next)
-
-            for r in range(group):
-                nr = (r + 1) % group
-                s_next = qk(kchunk(j), k, nr) if nr else qk(kchunk(j_next), k_next, 0)
-                cur = s_s[r]
-                s_s[nr] = s_next
-                soft_pv(k, r, cur, mx, vc_t[j])
-                mx = jnp.max(s_next, axis=0, keepdims=True)
+            k_next, half_next = first + tn // 2, tn % 2
+            tiles = group * tok // 256
+            for r in range(tiles):
+                if r + 1 < tiles:
+                    following = lambda u, r=r: qk(kc_s[pieces * half + u], k, pl.ds((r + 1) * 256, 256))
+                else:
+                    @pl.when(jnp.logical_and(first == 0, t == 0))
+                    def _():
+                        cache_chunk(2)
+                        cache_chunk(3)
+
+                    @pl.when(jnp.logical_and(half == 1, t < steps - 1))
+                    def _():
+                        arrived(QN, k_next)
+
+                    following = lambda u: qk(kc_s[pieces * half_next + u], k_next, pl.ds(0, 256))
+                mx = sub_step(r % 2, k, pl.ds(r * 256, 256), 256, mx, pieces, tok,
+                              lambda u: vc_t[2 * half + u // 2, :, (u % 2) * tok:(u % 2 + 1) * tok], following)
             return mx
 
-        lax.fori_loop(0, steps, step, jnp.max(s0, axis=0, keepdims=True))
-
-    cache_part(0, 6, True)
+        lax.fori_loop(0, steps, step, mx0)
+
+    wide_rows = group * tok // 2
+
+    def causal(h, val):
+        key = lax.broadcasted_iota(jnp.int32, (tok, wide_rows), 0)
+        row = (lax.broadcasted_iota(jnp.int32, (tok, wide_rows), 1) + h * wide_rows) & (tok - 1)
+        return jnp.where(key <= row, val, NEG)
+
+    def row_half(h):
+        return pl.ds(h * wide_rows, wide_rows)
 
     def new_block(k, carry):
         arrived(KN, k)
@@ -247,10 +305,6 @@
         vn_t[dev] = vn_raw[dev].T
         return carry
 
-    lax.fori_loop(0, NDEV, new_block, 0)
-    ahead = lax.broadcasted_iota(jnp.int32, (tok, tok), 0) <= lax.broadcasted_iota(jnp.int32, (tok, tok), 1)
-    half = pl.ds(0, tok)
-
     def send_out(k):
         return pltpu.make_async_remote_copy(src_ref=osend.at[k], dst_ref=o_s.at[k // 2, :, group_cols(c)], send_sem=osend_sem.at[k],
                                             recv_sem=orecv_sem.at[k], device_id=peer(k)[1], device_id_type=MESH_ID)
@@ -261,25 +315,27 @@
     def item(i):
         return i + 2 - (i // 6) * (2 * i - 5)
 
-    def phase2(i, carry):
+    def new_part(i, carry):
         k = item(i)
         p = peer(k)[0]
 
-        @pl.when(i // 2 == 2)
-        def _():
-            arrived(QN, k)
-            cache_part(k, 1, False)
-
-        s = jnp.where(ahead, qk(kn_s[p], k, 0), NEG)
-        s_s[0, half] = s
-        mx = jnp.max(s, axis=0, keepdims=True)
-        for r in range(group):
-            nr = (r + 1) % group
-            s_next = jnp.where(ahead, qk(kn_s[p], k, nr), NEG) if nr else qk(kn_s[0], k, 0)
-            cur = s_s[r, half]
-            s_s[nr, half] = s_next
-            soft_pv(k, r, cur, mx, vn_t[p])
-            mx = jnp.max(s_next, axis=0, keepdims=True)
+        @pl.when(jnp.logical_or(i == 0, i // 2 == 2))
+        def _():
+            @pl.when(i > 0)
+            def _():
+                arrived(QN, k)
+
+            cache_part((i // 4) * k, jnp.where(i == 0, 6, 1))
+
+        @pl.when(i == 0)
+        def _():
+            for cp in news:
+                cp.wait()
+            lax.fori_loop(0, NDEV, new_block, 0)
+
+        mx = first_tile(1, lambda u: causal(0, qk(kn_s[p], k, row_half(0))))
+        mx = sub_step(0, k, row_half(0), wide_rows, mx, 1, tok, lambda u: vn_t[p], lambda u: causal(1, qk(kn_s[p], k, row_half(1))))
+        mx = sub_step(1, k, row_half(1), wide_rows, mx, 1, tok, lambda u: vn_t[p], lambda u: qk(kn_s[0], k, row_half(0)))
 
         @pl.when(i > 0)
         def _():
@@ -287,14 +343,8 @@
 
         def earlier(j, mx):
             jn = jnp.minimum(j + 1, p - 1)
-            for r in range(group):
-                nr = (r + 1) % group
-                s_next = qk(kn_s[j], k, nr) if nr else qk(kn_s[jn], k, 0)
-                cur = s_s[r, half]
-                s_s[nr, half] = s_next
-                soft_pv(k, r, cur, mx, vn_t[j])
-                mx = jnp.max(s_next, axis=0, keepdims=True)
-            return mx
+            mx = sub_step(0, k, row_half(0), wide_rows, mx, 1, tok, lambda u: vn_t[j], lambda u: qk(kn_s[j], k, row_half(1)))
+            return sub_step(1, k, row_half(1), wide_rows, mx, 1, tok, lambda u: vn_t[j], lambda u: qk(kn_s[jn], k, row_half(0)))
 
         lax.fori_loop(0, p, earlier, mx)
         for r in range(group):
@@ -303,13 +353,14 @@
             osend[k, :, r * hd:(r + 1) * hd] = o_t.T.astype(jnp.bfloat16)
         return carry
 
-    lax.fori_loop(0, NDEV, phase2, 0)
+    arrived(QN, 0)
+    cache_chunk(0)
+    cache_chunk(1)
+    lax.fori_loop(0, NDEV, new_part, 0)
 
     own = pltpu.make_async_copy(osend.at[0], o_s.at[0, :, group_cols(c)], orecv_sem.at[0])
     for n in range(4):
         wo_tile(n).wait()
-    k_out.wait()
-    v_out.wait()
     quarter = tok // 4
 
     def y_piece(kc, old, last):
@@ -361,8 +412,8 @@
         y_copy(n).wait()
 
 
-def layer(x_loc, w_q, w_k, w_v, w_o, cos_f, sin_f, kc_t, vc_t):
-    kv_heads, tok, hd = kc_t.shape
+def layer(x_loc, w_q, w_k, w_v, w_o, table, kc_loc, vc_loc):
+    tok, kv_heads, hd = kc_loc.shape
     d_model = x_loc.shape[1]
     group = w_q.shape[1] // (kv_heads * hd)
     rows = group * tok
@@ -372,8 +423,8 @@
     dma = pltpu.SemaphoreType.DMA
     return pl.pallas_call(
         functools.partial(layer_kernel, group, tok, hd ** -0.5),
-        out_shape=(sds((tok, d_model), bf), sds((tok, kv_heads * hd), bf), sds((tok, kv_heads * hd), bf)),
-        in_specs=[hbm] * 9,
+        out_shape=(sds((tok, d_model), bf), sds((kv_heads, tok, hd), bf), sds((kv_heads, tok, hd), bf)),
+        in_specs=[hbm] * 8,
         out_specs=(hbm, hbm, hbm),
         scratch_shapes=[
             pltpu.VMEM((tok, d_model), bf),
@@ -393,10 +444,12 @@
             pltpu.VMEM((NDEV, hd, rows), f32),
             pltpu.VMEM((NDEV, 1, rows), f32),
             pltpu.VMEM((NDEV, 1, rows), f32),
-            pltpu.VMEM((group, 2 * tok, tok), f32),
+            pltpu.VMEM((2, 2, 4 * tok, 128), f32),
             pltpu.VMEM((NDEV, tok, group * hd), bf),
             pltpu.VMEM((NDEV // 2, tok, 2 * group * hd), bf),
-            dma((3,)),
+            pltpu.VMEM((NDEV, tok, hd), bf),
+            pltpu.VMEM((NDEV, tok, hd), bf),
+            dma((4,)),
             dma((NBUF,)),
             dma((5, NDEV)),
             dma((5, NDEV)),
@@ -405,22 +458,18 @@
         ],
         compiler_params=pltpu.CompilerParams(collective_id=0, has_side_effects=True, vmem_limit_bytes=63 * 2**20),
         name='head_layer',
-    )(x_loc, w_q, w_k, w_v, w_o, cos_f, sin_f, kc_t, vc_t)
+    )(x_loc, w_q, w_k, w_v, w_o, table, kc_loc.reshape(kv_heads, tok, hd), vc_loc.reshape(kv_heads, tok, hd))
 
 
 def solution(mesh):
     seq_size = mesh.shape['sp'] * mesh.shape['cp']
-    cp_size = mesh.shape['cp']
     row_spec = P(('dp', 'sp', 'cp'))
 
     def local_fn(x_loc, kc_loc, vc_loc, w_q, w_k, w_v, w_o):
         tok, d_model = x_loc.shape
         cache_loc, kv_heads, hd = kc_loc.shape
-        seq_idx = lax.axis_index('sp') * cp_size + lax.axis_index('cp')
-        kc_t = jnp.transpose(kc_loc, (1, 0, 2))
-        vc_t = jnp.transpose(vc_loc, (1, 0, 2))
-        cos_f, sin_f = rope_tables(cache_loc * seq_size + seq_idx * tok + jnp.arange(tok), hd)
-        y_loc, k_rows, v_rows = layer(x_loc, w_q, w_k, w_v, w_o, cos_f, sin_f, kc_t, vc_t)
+        table = jnp.asarray(rope_table(cache_loc * seq_size, tok * seq_size, hd))
+        y_loc, k_rows, v_rows = layer(x_loc, w_q, w_k, w_v, w_o, table, kc_loc, vc_loc)
         return y_loc, k_rows.reshape(tok, kv_heads, hd), v_rows.reshape(tok, kv_heads, hd)
 
     return jax.shard_map(local_fn, mesh=mesh, in_specs=(row_spec, row_spec, row_spec, P(), P(), P(), P()), out_specs=(row_spec, row_spec, row_spec), check_vma=False)

time: 145 us -> 140 us (0.966)
  local copies, waits for them, and re-layouts: 9.99 us -> 5.85 us
  other arithmetic: 1.84 us -> 0 us
    transpose x1 -> x0, local copies, waits for them, and re-layouts: 3.23 us -> none  [local_fn(): vc_t = jnp.transpose(vc_loc, (1, 0, 2))]
    mul x1 -> x0, other arithmetic: 1.83 us -> none  [rope_tables(): return (jnp.cos(angles), jnp.sin(angles) * sign)]
    unnamed x5 -> x7, local copies, waits for them, and re-layouts: 6.76 us -> 5.85 us
where the time goes in v4:
time: 140 us; the launch traced here: 139 us
  Pallas kernels  132 us (94%)
  local copies, waits for them, and re-layouts  5.85 us (4%)
    pallas_call x1, Pallas kernels, layer(): pl.pallas_call(functools.partial(layer_kernel, group, tok, hd ** (-0.5)),...  132 us
    unnamed x7, local copies, waits for them, and re-layouts  5.85 us

profile of v4, /device:TPU:0, one launch (start us, length us, event | category | flops | bytes accessed | tf_op | source)
XLA Modules:
  0.0 139.0 jit_solution(3358176963782806903)
XLA Ops:
  0.6 132.5 %head_layer.1 = (bf16[512,3072]{1,0:T(8,128)(2,1)}, bf16[8,512,128]{2,1,0:T(8,128)(2,1)}, bf16[8,512,128]{2,1,0:T(8,128)(2,1)}) custom-call(bf16[512,3072]{1,0:T(8,128)(2,1)} %x_hbm.1, bf16[3072,3072]{1,0:T(8,128)(2,1)} %wq_hbm.1, bf16[3072,1024]{1,0:T(8,128)(2,1)} %wk_hbm.1, bf16[3072,1024]{1,0:T(8,128)(2,1)} %wv_hbm.1, bf16[3072,3072]{1,0:T(8,128)(2,1)} %wo_hbm.1, ...), custom_call_target="tpu_custom_call" | custom-call | tf_op jit(solution)/shard_map/head_layer/pallas_call | solution.py:424
  133.1 0.0 copy-start.1
  133.1 0.0 copy-start
  133.2 3.9 %copy.14 = bf16[512,3072]{1,0:T(8,128)(2,1)} copy(bf16[512,3072]{1,0:T(8,128)(2,1)} %get-tuple-element.12) | data formatting | bytes 6291456
  137.1 0.0 copy-done.1
  137.1 1.0 copy.15
  138.0 0.0 copy-done
  138.0 1.0 copy.16
Async XLA Ops:
  133.1 3.9 %copy-start.1 = (bf16[8,512,128]{2,1,0:T(8,128)(2,1)S(1)}, bf16[8,512,128]{2,1,0:T(8,128)(2,1)}, u32[]{:S(2)}) copy-start(bf16[8,512,128]{2,1,0:T(8,128)(2,1)} %get-tuple-element.7) | copy-start | bytes 3145732
  133.1 4.9 %copy-start = (bf16[8,512,128]{2,1,0:T(8,128)(2,1)S(1)}, bf16[8,512,128]{2,1,0:T(8,128)(2,1)}, u32[]{:S(2)}) copy-start(bf16[8,512,128]{2,1,0:T(8,128)(2,1)} %get-tuple-element.8) | copy-start | bytes 3145732

commit v5 on v4

--- a/solution.py
+++ b/solution.py
@@ -313,7 +313,7 @@
         pltpu.make_async_copy(osend.at[k], o_s.at[k // 2, :, group_cols(peer(k)[0] % 2)], orecv_sem.at[k]).wait()
 
     def item(i):
-        return i + 2 - (i // 6) * (2 * i - 5)
+        return jnp.where(i < 4, 2 + 2 * (i % 2) + i // 2, jnp.where(i < 6, i + 2, NDEV - 1 - i))
 
     def new_part(i, carry):
         k = item(i)

time: 140 us -> 140 us (level)
  no operation moved by 1% of the time
where the time goes in v5:
time: 140 us; the launch traced here: 139 us
  Pallas kernels  132 us (94%)
  local copies, waits for them, and re-layouts  5.85 us (4%)
    pallas_call x1, Pallas kernels, layer(): pl.pallas_call(functools.partial(layer_kernel, group, tok, hd ** (-0.5)),...  132 us
    unnamed x7, local copies, waits for them, and re-layouts  5.85 us

profile of v5, /device:TPU:0, one launch (start us, length us, event | category | flops | bytes accessed | tf_op | source)
XLA Modules:
  0.0 138.9 jit_solution(16076540556785002079)
XLA Ops:
  0.6 132.4 %head_layer.1 = (bf16[512,3072]{1,0:T(8,128)(2,1)}, bf16[8,512,128]{2,1,0:T(8,128)(2,1)}, bf16[8,512,128]{2,1,0:T(8,128)(2,1)}) custom-call(bf16[512,3072]{1,0:T(8,128)(2,1)} %x_hbm.1, bf16[3072,3072]{1,0:T(8,128)(2,1)} %wq_hbm.1, bf16[3072,1024]{1,0:T(8,128)(2,1)} %wk_hbm.1, bf16[3072,1024]{1,0:T(8,128)(2,1)} %wv_hbm.1, bf16[3072,3072]{1,0:T(8,128)(2,1)} %wo_hbm.1, ...), custom_call_target="tpu_custom_call" | custom-call | tf_op jit(solution)/shard_map/head_layer/pallas_call | solution.py:424
  133.1 0.0 copy-start.1
  133.1 0.0 copy-start
  133.1 3.9 %copy.14 = bf16[512,3072]{1,0:T(8,128)(2,1)} copy(bf16[512,3072]{1,0:T(8,128)(2,1)} %get-tuple-element.12) | data formatting | bytes 6291456
  137.0 0.0 copy-done.1
  137.0 1.0 copy.15
  138.0 0.0 copy-done
  138.0 1.0 copy.16
Async XLA Ops:
  133.1 3.9 %copy-start.1 = (bf16[8,512,128]{2,1,0:T(8,128)(2,1)S(1)}, bf16[8,512,128]{2,1,0:T(8,128)(2,1)}, u32[]{:S(2)}) copy-start(bf16[8,512,128]{2,1,0:T(8,128)(2,1)} %get-tuple-element.7) | copy-start | bytes 3145732
  133.1 4.9 %copy-start = (bf16[8,512,128]{2,1,0:T(8,128)(2,1)S(1)}, bf16[8,512,128]{2,1,0:T(8,128)(2,1)}, u32[]{:S(2)}) copy-start(bf16[8,512,128]{2,1,0:T(8,128)(2,1)} %get-tuple-element.8) | copy-start | bytes 3145732
